TPU v7x, 64 devices: a 2x2x8 block of a 4x4x8 slice. The times are simulated.
64 devices in a mesh: data: 4 (over x, y), model: 16 (over z, core).
Axes of the slice: x: 2, y: 2, z: 8, core: 2. Of those that a mesh axis runs over, the one named last changes fastest.
The devices are a block of a 4x4x8 slice.
Arguments:
- resid_x: bfloat16 [16384, 2048], P('data'), parts along dimension 0
- ln_mean: float32 [16384], P('data'), parts along dimension 0
- ln_rstd: float32 [16384], P('data'), parts along dimension 0
- ln_gain: bfloat16 [2048], replicated
- grad_y: bfloat16 [16384, 2048], P('data'), parts along dimension 0
- w_qkv: bfloat16 [2048, 6144], P(None, 'model')
- w_out: bfloat16 [16, 128, 2048], P('model')
- w_up: bfloat16 [2048, 8192], P(None, 'model')
- w_down: bfloat16 [8192, 2048], P('model')
Outputs:
- output 1: bfloat16 [16384, 2048], P('data'), parts along dimension 0
- output 2: bfloat16 [8192, 6144], P('data', 'model'), parts along dimension 0
- output 3: bfloat16 [64, 128, 2048], P(('data', 'model')), parts along dimension 0
- output 4: bfloat16 [8192, 8192], P('data', 'model'), parts along dimension 0
- output 5: bfloat16 [32768, 2048], P(('data', 'model')), parts along dimension 0
There are 4 independent parts. A program takes and returns all parts, laid end to end along the dimension named above; an argument that names none is the same for every part.
All inputs are finite; a program needn't handle non-finite values.
Results may differ from a plain program's by a relative error of at most 0.0168419.
Values are sent between devices in bfloat16 or wider.
A program may use at most 768 MiB of HBM per device.

v0:
```python
import jax
import jax.numpy as jnp
from jax import lax
from jax.sharding import PartitionSpec as P

CONTRACT_ROWS = (((0,), (0,)), ((), ()))
CONTRACT_COLS = (((1,), (1,)), ((), ()))


def rope_tables(tokens, rot_dim):
    half_rot = rot_dim // 2
    positions = jnp.arange(tokens, dtype=jnp.float32)[:, None]
    inv_freq = jnp.power(10000.0, -2.0 * jnp.arange(half_rot, dtype=jnp.float32) / rot_dim)
    angles = positions * inv_freq[None, :]
    return jnp.cos(angles)[:, None, :], jnp.sin(angles)[:, None, :]


def rotate(vectors, rope_cos, rope_sin):
    half_rot = rope_cos.shape[-1]
    first_half = vectors[..., :half_rot]
    second_half = vectors[..., half_rot:2 * half_rot]
    return jnp.concatenate([first_half * rope_cos - second_half * rope_sin, second_half * rope_cos + first_half * rope_sin, vectors[..., 2 * half_rot:]], axis=-1)


def exact_gelu(pre_act):
    return jax.nn.gelu(pre_act, approximate=False)


def attention_pair(q_rot, k_rot, values, d_attn):
    tokens = q_rot.shape[-3]
    att_scale = q_rot.shape[-1] ** -0.5
    scores = jnp.einsum("...qhd,...khd->...hqk", q_rot, k_rot, preferred_element_type=jnp.float32) * att_scale
    causal = jnp.arange(tokens)[:, None] >= jnp.arange(tokens)[None, :]
    attn_probs = jax.nn.softmax(jnp.where(causal, scores, -1e30), axis=-1)
    probs_bf = attn_probs.astype(jnp.bfloat16)
    attn_out = jnp.einsum("...hqk,...khd->...qhd", probs_bf, values, preferred_element_type=jnp.float32).astype(jnp.bfloat16)
    d_probs = jnp.einsum("...qhd,...khd->...hqk", d_attn, values, preferred_element_type=jnp.float32)
    d_values = jnp.einsum("...hqk,...qhd->...khd", probs_bf, d_attn, preferred_element_type=jnp.float32)
    row_delta = jnp.sum(attn_probs * d_probs, axis=-1, keepdims=True)
    d_scores = (attn_probs * (d_probs - row_delta) * att_scale).astype(jnp.bfloat16)
    d_q_rot = jnp.einsum("...hqk,...khd->...qhd", d_scores, k_rot, preferred_element_type=jnp.float32)
    d_k_rot = jnp.einsum("...hqk,...qhd->...khd", d_scores, q_rot, preferred_element_type=jnp.float32)
    return attn_out, d_q_rot, d_k_rot, d_values


def ln_backward(d_normed, x_hat, gain_f32, ln_rstd, grad_y):
    d_hat = d_normed * gain_f32
    mean_d = jnp.mean(d_hat, axis=-1, keepdims=True)
    mean_dx = jnp.mean(d_hat * x_hat, axis=-1, keepdims=True)
    grad_in = ln_rstd[:, None] * (d_hat - mean_d - x_hat * mean_dx)
    return (grad_y.astype(jnp.float32) + grad_in).astype(jnp.bfloat16)


def solution(mesh):
    def device_step(resid_x, ln_mean, ln_rstd, ln_gain, grad_y, w_qkv, w_out, w_up, w_down):
        heads_local = w_out.shape[0]
        head_dim = w_out.shape[1]
        tokens = resid_x.shape[0]
        x_hat = (resid_x.astype(jnp.float32) - ln_mean[:, None]) * ln_rstd[:, None]
        gain_f32 = ln_gain.astype(jnp.float32)
        normed = (x_hat * gain_f32).astype(jnp.bfloat16)
        qkv_proj = jnp.dot(normed, w_qkv, preferred_element_type=jnp.float32).reshape(tokens, heads_local, 3, head_dim)
        rope_cos, rope_sin = rope_tables(tokens, head_dim // 4)
        q_rot = rotate(qkv_proj[..., 0, :], rope_cos, rope_sin).astype(jnp.bfloat16)
        k_rot = rotate(qkv_proj[..., 1, :], rope_cos, rope_sin).astype(jnp.bfloat16)
        values = qkv_proj[..., 2, :].astype(jnp.bfloat16)
        d_attn = jnp.einsum("te,hde->thd", grad_y, w_out, preferred_element_type=jnp.float32).astype(jnp.bfloat16)
        attn_out, d_q_rot, d_k_rot, d_values = attention_pair(q_rot, k_rot, values, d_attn)
        d_qkv = jnp.stack([rotate(d_q_rot, rope_cos, -rope_sin), rotate(d_k_rot, rope_cos, -rope_sin), d_values], axis=-2)
        d_qkv = d_qkv.astype(jnp.bfloat16).reshape(tokens, w_qkv.shape[1])
        grad_w_qkv = lax.dot_general(normed, d_qkv, CONTRACT_ROWS, preferred_element_type=jnp.float32).astype(jnp.bfloat16)
        grad_w_out = jnp.einsum("thd,te->hde", attn_out, grad_y, preferred_element_type=jnp.float32).astype(jnp.bfloat16)
        pre_act = jnp.dot(normed, w_up, preferred_element_type=jnp.float32)
        act_out, gelu_vjp = jax.vjp(exact_gelu, pre_act)
        act_bf = act_out.astype(jnp.bfloat16)
        grad_w_down = lax.dot_general(act_bf, grad_y, CONTRACT_ROWS, preferred_element_type=jnp.float32).astype(jnp.bfloat16)
        d_act = lax.dot_general(grad_y, w_down, CONTRACT_COLS, preferred_element_type=jnp.float32)
        d_pre = gelu_vjp(d_act)[0].astype(jnp.bfloat16)
        grad_w_up = lax.dot_general(normed, d_pre, CONTRACT_ROWS, preferred_element_type=jnp.float32).astype(jnp.bfloat16)
        part_sum = lax.dot_general(d_pre, w_up, CONTRACT_COLS, preferred_element_type=jnp.float32) + lax.dot_general(d_qkv, w_qkv, CONTRACT_COLS, preferred_element_type=jnp.float32)
        d_normed = lax.psum(part_sum.astype(jnp.bfloat16), "model").astype(jnp.float32)
        grad_x = ln_backward(d_normed, x_hat, gain_f32, ln_rstd, grad_y)
        return grad_x, grad_w_qkv, grad_w_out, grad_w_up, grad_w_down

    in_specs = (P("data", None), P("data"), P("data"), P(None), P("data", None), P(None, "model"), P("model", None, None), P(None, "model"), P("model", None))
    out_specs = (P("data", None), P("data", "model"), P(("data", "model"), None, None), P("data", "model"), P(("data", "model"), None))
    return jax.shard_map(device_step, mesh=mesh, in_specs=in_specs, out_specs=out_specs, check_vma=False)
```

profile of v0, /device:TPU:21, one launch (start us, length us, event | category | flops | bytes accessed | tf_op | source)
XLA Modules:
  0.0 590.8 jit_solution(13371557452263543189)
XLA Ops:
  7.3 0.8 convert_element_type.91
  8.1 0.6 copy-done.23
  8.7 15.9 %multiply_convert_fusion.1 = bf16[4096,2048]{1,0:T(8,128)(2,1)} fusion(bf16[4096,2048]{1,0:T(8,128)(2,1)} %param.9, f32[2048]{0:T(1024)S(1)} %convert_element_type.91, f32[4096]{0:T(1024)} %param.10, f32[4096]{0:T(1024)} %param.11), kind=kLoop, calls=%fused_computation.13 | loop fusion | flops 41943040 | bytes 33595392 | tf_op jit(solution)/shard_map/convert_element_type | solution.py:61
  24.7 10.8 %fusion.64 = f32[4096,384]{0,1:T(8,128)S(1)} fusion(bf16[4096,2048]{1,0:T(8,128)(2,1)} %multiply_convert_fusion.1, bf16[2048,384]{1,0:T(8,128)(2,1)S(1)} %copy-done.8), kind=kOutput, calls=%fused_computation.94 | convolution fusion | flops 6442450944 | bytes 24641536 | tf_op jit(solution)/shard_map/dot_general | solution.py:62
  35.4 0.5 slice_bitcast_fusion.1
  35.9 2.1 copy-done.7
  38.0 0.2 fusion.39
  38.3 1.3 fusion.50
  39.6 24.2 %fusion.2 = (f32[4096]{0:T(1024)S(1)}, f32[4096,4096]{0,1:T(8,128)}) fusion(bf16[4096,96]{0,1:T(8,128)(2,1)S(1)} %get-tuple-element.27, bf16[4096,16]{0,1:T(8,128)(2,1)S(1)} %get-tuple-element.16, bf16[4096,16]{0,1:T(8,128)(2,1)S(1)} %get-tuple-element.15, bf16[4096,96]{0,1:T(8,128)(2,1)S(1)} %get-tuple-element.28, ...), kind=kOutput, calls=%fused_computation.7 | convolution fusion | flops 4368363520 | bytes 69222400 | tf_op jit(solution)/shard_map/...qhd,...khd->...hqk/dot_general | solution.py:32
  63.9 21.8 %fusion.1 = f32[4096]{0:T(1024)S(1)} fusion(f32[4096,4096]{0,1:T(8,128)} %get-tuple-element.24, f32[4096]{0:T(1024)S(1)} %get-tuple-element.23), kind=kLoop, calls=%fused_computation.6 | loop fusion | flops 83881984 | bytes 67141632 | tf_op jit(solution)/shard_map/reduce_sum | solution.py:34
  85.7 8.4 %convolution_convert_fusion = bf16[4096,128]{1,0:T(8,128)(2,1)S(1)} fusion(bf16[4096,2048]{1,0:T(8,128)(2,1)} %param.13, bf16[1,128,2048]{2,1,0:T(8,128)(2,1)S(1)} %copy-done.32), kind=kOutput, calls=%fused_computation.40 | convolution fusion | flops 2148007936 | bytes 18350080 | tf_op jit(solution)/shard_map/te,hde->thd/dot_general | solution.py:67
  94.2 49.3 %multiply_reduce_fusion = (f32[4096]{0:T(1024)S(1)}, f32[4096,4096]{0,1:T(8,128)}) fusion(f32[4096]{0:T(1024)S(1)} %fusion.1, f32[4096]{0:T(1024)S(1)} %get-tuple-element.23, f32[4096,4096]{0,1:T(8,128)} %get-tuple-element.24, bf16[4096,128]{1,0:T(8,128)(2,1)S(1)} %convolution_convert_fusion, f32[4096,1,3,128]{0,3,2,1:T(8,128)} %bitcast.87), kind=kOutput, calls=%fused_computation.1 | convolution fusion | flops 4412403712 | bytes 136364032 | tf_op jit(solution)/shard_map/...qhd,...khd->...hqk/dot_general | solution.py:37
  143.5 53.6 %multiply_convert_fusion = bf16[4096,4096]{0,1:T(8,128)(2,1)} fusion(f32[4096,4096]{0,1:T(8,128)} %get-tuple-element.26, f32[4096]{0:T(1024)S(1)} %get-tuple-element.25, f32[4096]{0:T(1024)S(1)} %fusion.1, f32[4096]{0:T(1024)S(1)} %get-tuple-element.23, f32[4096,4096]{0,1:T(8,128)} %get-tuple-element.24), kind=kLoop, calls=%fused_computation | loop fusion | flops 150994944 | bytes 167821312 | tf_op jit(solution)/shard_map/convert_element_type | solution.py:40
  197.1 13.0 %convolution_bitcast_fusion.1 = f32[4096,1,128]{0,2,1:T(8,128)S(1)} fusion(bf16[4096,4096]{0,1:T(8,128)(2,1)} %multiply_convert_fusion, bf16[4096,96]{0,1:T(8,128)(2,1)S(1)} %copy-done.6, bf16[4096,16]{0,1:T(8,128)(2,1)S(1)} %copy-done.16, bf16[4096,16]{0,1:T(8,128)(2,1)S(1)} %copy-done.14), kind=kOutput, calls=%fused_computation.37 | convolution fusion | flops 4298113024 | bytes 36700160 | tf_op jit(solution)/shard_map/...hqk,...khd->...qhd/dot_general | solution.py:41
  210.1 16.5 %convolution_bitcast_fusion = f32[4096,1,128]{0,2,1:T(8,128)S(1)} fusion(bf16[4096,4096]{0,1:T(8,128)(2,1)} %multiply_convert_fusion, bf16[4096,96]{0,1:T(8,128)(2,1)} %copy-done.4, bf16[4096,16]{0,1:T(8,128)(2,1)S(1)} %copy-done.10, bf16[4096,16]{0,1:T(8,128)(2,1)S(1)} %copy-done.12), kind=kOutput, calls=%fused_computation.36 | convolution fusion | flops 4298113024 | bytes 36700160 | tf_op jit(solution)/shard_map/...hqk,...qhd->...khd/dot_general | solution.py:42
  226.6 1.0 slice.129
  227.6 1.9 subtract_convert_fusion.1
  229.5 1.0 slice.128
  230.5 28.8 %fusion.20 = bf16[4096,1,1,128]{0,3,2,1:T(8,128)(2,1)S(1)} fusion(bf16[4096,128]{1,0:T(8,128)(2,1)} %copy-done.33, f32[4096,4096]{0,1:T(8,128)} %get-tuple-element.24, f32[4096]{0:T(1024)S(1)} %fusion.1, f32[4096]{0:T(1024)S(1)} %get-tuple-element.23), kind=kOutput, calls=%fused_computation.41 | convolution fusion | flops 4396154880 | bytes 69238784 | tf_op jit(solution)/shard_map/...hqk,...qhd->...khd/dot_general | solution.py:38
  259.4 12.0 %fusion.62 = f32[4096,512]{1,0:T(8,128)S(1)} fusion(bf16[4096,2048]{1,0:T(8,128)(2,1)} %multiply_convert_fusion.1, bf16[2048,512]{1,0:T(8,128)(2,1)S(1)} %copy-done), kind=kOutput, calls=%fused_computation.92 | convolution fusion | flops 8589934592 | bytes 27262976 | tf_op jit(solution)/shard_map/dot_general | solution.py:73
  271.4 33.1 %add_convert_fusion.2 = (bf16[4096,512]{1,0:T(8,128)(2,1)S(1)}, f32[4096,512]{1,0:T(8,128)}) fusion(f32[4096,512]{1,0:T(8,128)S(1)} %fusion.62, bf16[4096,2048]{1,0:T(8,128)(2,1)} %param.13, bf16[512,2048]{1,0:T(8,128)(2,1)S(1)} %copy-done.31), kind=kOutput, calls=%fused_computation.22 | convolution fusion | flops 8740929536 | bytes 39845888 | tf_op jit(solution)/shard_map/dot_general | solution.py:77
  304.7 14.5 %fusion.63 = f32[4096,2048]{1,0:T(8,128)} fusion(bf16[4096,512]{1,0:T(8,128)(2,1)S(1)} %get-tuple-element.7, bf16[2048,512]{1,0:T(8,128)(2,1)S(1)} %copy-done), kind=kOutput, calls=%fused_computation.93 | convolution fusion | flops 8589934592 | bytes 39845888 | tf_op jit(solution)/shard_map/dot_general | solution.py:80
  319.2 0.1 maximum_bitcast_fusion
  319.4 2.0 pad_maximum_fusion
  321.4 22.3 %add_convert_fusion.1 = bf16[4096,2048]{1,0:T(8,128)(2,1)} fusion(f32[4096,2048]{1,0:T(8,128)} %fusion.63, bf16[4096,384]{0,1:T(8,128)(2,1)} %bitcast.84, bf16[2048,384]{1,0:T(8,128)(2,1)} %param.14), kind=kOutput, calls=%fused_computation.12 | convolution fusion | flops 6459228160 | bytes 55050240 | tf_op jit(solution)/shard_map/dot_general | solution.py:80
  343.8 14.6 %convolution_convert_fusion.2 = bf16[2048,384]{1,0:T(8,128)(2,1)} fusion(bf16[4096,2048]{1,0:T(8,128)(2,1)} %multiply_convert_fusion.1, bf16[4096,384]{0,1:T(8,128)(2,1)} %bitcast.85), kind=kOutput, calls=%fused_computation.49 | convolution fusion | flops 6443237376 | bytes 21495808 | tf_op jit(solution)/shard_map/dot_general | solution.py:71
  358.4 13.4 %convolution_convert_fusion.1 = bf16[2048,512]{1,0:T(8,128)(2,1)} fusion(bf16[4096,2048]{1,0:T(8,128)(2,1)} %multiply_convert_fusion.1, bf16[4096,512]{1,0:T(8,128)(2,1)S(1)} %copy-done.35), kind=kOutput, calls=%fused_computation.48 | convolution fusion | flops 8590983168 | bytes 23068672 | tf_op jit(solution)/shard_map/dot_general | solution.py:79
  371.8 18.6 %fusion.31 = bf16[512,2048]{1,0:T(8,128)(2,1)} fusion(bf16[4096,2048]{1,0:T(8,128)(2,1)} %param.13, f32[4096,512]{1,0:T(8,128)} %get-tuple-element.8, f32[4096,512]{1,0:T(8,128)} %copy-done.1), kind=kOutput, calls=%fused_computation.47 | convolution fusion | flops 8597274624 | bytes 35651584 | tf_op jit(solution)/shard_map/dot_general | solution.py:76
  390.5 33.8 %fusion.35 = bf16[1,128,2048]{2,1,0:T(8,128)(2,1)} fusion(bf16[4096,2048]{1,0:T(8,128)(2,1)} %param.13, f32[4096,1,3,128]{0,3,2,1:T(8,128)} %bitcast.88, f32[4096,4096]{0,1:T(8,128)} %get-tuple-element.24, f32[4096]{0:T(1024)S(1)} %copy-done.28, f32[4096]{0:T(1024)S(1)} %copy-done.26), kind=kOutput, calls=%fused_computation.51 | convolution fusion | flops 6543900672 | bytes 85491712 | tf_op jit(solution)/shard_map/thd,te->hde/dot_general | solution.py:72
  424.3 116.7 %all-reduce.2.cloned.1.call-done = bf16[4096,2048]{1,0:T(8,128)(2,1)} async-done(((bf16[4096,2048]{1,0:T(8,128)(2,1)}), bf16[4096,2048]{1,0:T(8,128)(2,1)}) %all-reduce.2.cloned.1.call-update) | async-done | bytes 16777232 | tf_op jit(solution)/shard_map/psum | solution.py:81
  541.0 16.2 %fusion.3 = (f32[4096]{0:T(1024)S(1)}, f32[4096]{0:T(1024)S(1)}) fusion(bf16[4096,2048]{1,0:T(8,128)(2,1)} %all-reduce.2.cloned.1.call-done, f32[2048]{0:T(1024)S(1)} %copy-done.24, f32[4096]{0:T(1024)S(1)} %copy-done.22, f32[4096]{0:T(1024)S(1)} %copy-done.21, bf16[4096,2048]{1,0:T(8,128)(2,1)} %param.9), kind=kLoop, calls=%fused_computation.11 | loop fusion | flops 67100672 | bytes 33628160 | tf_op jit(solution)/shard_map/reduce_sum | solution.py:48
  557.2 26.3 %add_convert_fusion = bf16[4096,2048]{1,0:T(8,128)(2,1)} fusion(bf16[4096,2048]{1,0:T(8,128)(2,1)} %all-reduce.2.cloned.1.call-done, bf16[4096,2048]{1,0:T(8,128)(2,1)} %param.9, bf16[4096,2048]{1,0:T(8,128)(2,1)} %param.13, f32[4096]{0:T(1024)S(1)} %broadcast_multiply_fusion, f32[4096]{0:T(1024)S(1)} %broadcast_multiply_fusion.1, f32[2048]{0:T(1024)S(1)} %copy-done.24, ...), kind=kLoop, calls=%fused_computation.8 | loop fusion | flops 100663296 | bytes 67182592 | tf_op jit(solution)/shard_map/convert_element_type | solution.py:51
  (76 shorter events, 0.4 us)
Async XLA Ops:
  7.2 252.2 %copy-start = (bf16[2048,512]{1,0:T(8,128)(2,1)S(1)}, bf16[2048,512]{1,0:T(8,128)(2,1)}, u32[]{:S(2)}) copy-start(bf16[2048,512]{1,0:T(8,128)(2,1)} %param.16) | copy-start | bytes 6291460
  7.2 533.8 %all-reduce.2.cloned.1.call-start = ((), (), s32[]{:S(2)}) async-start(), calls=%async_computation | async-start | bytes 33554432 | tf_op jit(solution)/shard_map/psum | solution.py:81
  7.3 30.9 %copy-start.29 = (f32[16]{0:T(128)}, f32[16]{0:T(128)S(1)}, u32[]{:S(2)}) copy-start(f32[16]{0:T(128)S(1)} %multiply_power_fusion) | copy-start | bytes 196
  8.7 16.0 %copy-start.8 = (bf16[2048,384]{1,0:T(8,128)(2,1)S(1)}, bf16[2048,384]{1,0:T(8,128)(2,1)}, u32[]{:S(2)}) copy-start(bf16[2048,384]{1,0:T(8,128)(2,1)} %param.14) | copy-start | bytes 4718596
  38.2 25.6 %copy-start.4 = (bf16[4096,96]{0,1:T(8,128)(2,1)}, bf16[4096,96]{0,1:T(8,128)(2,1)S(1)}, u32[]{:S(2)}) copy-start(bf16[4096,96]{0,1:T(8,128)(2,1)S(1)} %get-tuple-element.28) | copy-start | bytes 2359300
  38.2 25.6 %copy-start.5 = (bf16[4096,96]{0,1:T(8,128)(2,1)}, bf16[4096,96]{0,1:T(8,128)(2,1)S(1)}, u32[]{:S(2)}) copy-start(bf16[4096,96]{0,1:T(8,128)(2,1)S(1)} %get-tuple-element.27) | copy-start | bytes 2359300
  39.5 24.3 %copy-start.9 = (bf16[4096,16]{0,1:T(8,128)(2,1)}, bf16[4096,16]{0,1:T(8,128)(2,1)S(1)}, u32[]{:S(2)}) copy-start(bf16[4096,16]{0,1:T(8,128)(2,1)S(1)} %get-tuple-element.21) | copy-start | bytes 393220
  39.6 24.3 %copy-start.11 = (bf16[4096,16]{0,1:T(8,128)(2,1)}, bf16[4096,16]{0,1:T(8,128)(2,1)S(1)}, u32[]{:S(2)}) copy-start(bf16[4096,16]{0,1:T(8,128)(2,1)S(1)} %get-tuple-element.22) | copy-start | bytes 393220
  39.6 24.3 %copy-start.13 = (bf16[4096,16]{0,1:T(8,128)(2,1)}, bf16[4096,16]{0,1:T(8,128)(2,1)S(1)}, u32[]{:S(2)}) copy-start(bf16[4096,16]{0,1:T(8,128)(2,1)S(1)} %get-tuple-element.15) | copy-start | bytes 393220
  39.6 24.3 %copy-start.15 = (bf16[4096,16]{0,1:T(8,128)(2,1)}, bf16[4096,16]{0,1:T(8,128)(2,1)S(1)}, u32[]{:S(2)}) copy-start(bf16[4096,16]{0,1:T(8,128)(2,1)S(1)} %get-tuple-element.16) | copy-start | bytes 393220
  63.8 166.7 %copy-start.25 = (f32[4096]{0:T(1024)}, f32[4096]{0:T(1024)S(1)}, u32[]{:S(2)}) copy-start(f32[4096]{0:T(1024)S(1)} %get-tuple-element.23) | copy-start | bytes 49156
  63.9 21.8 %copy-start.32 = (bf16[1,128,2048]{2,1,0:T(8,128)(2,1)S(1)}, bf16[1,128,2048]{2,1,0:T(8,128)(2,1)}, u32[]{:S(2)}) copy-start(bf16[1,128,2048]{2,1,0:T(8,128)(2,1)} %param.15) | copy-start | bytes 1572868
  85.7 144.8 %copy-start.27 = (f32[4096]{0:T(1024)}, f32[4096]{0:T(1024)S(1)}, u32[]{:S(2)}) copy-start(f32[4096]{0:T(1024)S(1)} %fusion.1) | copy-start | bytes 49156
  94.1 49.3 %copy-start.33 = (bf16[4096,128]{1,0:T(8,128)(2,1)}, bf16[4096,128]{1,0:T(8,128)(2,1)S(1)}, u32[]{:S(2)}) copy-start(bf16[4096,128]{1,0:T(8,128)(2,1)S(1)} %convolution_convert_fusion) | copy-start | bytes 3145732
  143.5 53.6 %copy-start.6 = (bf16[4096,96]{0,1:T(8,128)(2,1)S(1)}, bf16[4096,96]{0,1:T(8,128)(2,1)}, u32[]{:S(2)}) copy-start(bf16[4096,96]{0,1:T(8,128)(2,1)} %copy-done.5) | copy-start | bytes 2359300
  143.5 53.6 %copy-start.14 = (bf16[4096,16]{0,1:T(8,128)(2,1)S(1)}, bf16[4096,16]{0,1:T(8,128)(2,1)}, u32[]{:S(2)}) copy-start(bf16[4096,16]{0,1:T(8,128)(2,1)} %copy-done.13) | copy-start | bytes 393220
  143.5 53.6 %copy-start.16 = (bf16[4096,16]{0,1:T(8,128)(2,1)S(1)}, bf16[4096,16]{0,1:T(8,128)(2,1)}, u32[]{:S(2)}) copy-start(bf16[4096,16]{0,1:T(8,128)(2,1)} %copy-done.15) | copy-start | bytes 393220
  210.1 17.5 %copy-start.30 = (f32[16]{0:T(128)S(1)}, f32[16]{0:T(128)}, u32[]{:S(2)}) copy-start(f32[16]{0:T(128)} %copy-done.29) | copy-start | bytes 196
  271.4 33.2 %copy-start.1 = (f32[4096,512]{1,0:T(8,128)}, f32[4096,512]{1,0:T(8,128)S(1)}, u32[]{:S(2)}) copy-start(f32[4096,512]{1,0:T(8,128)S(1)} %fusion.62) | copy-start | bytes 25165828
  304.6 14.6 %copy-start.34 = (bf16[4096,512]{1,0:T(8,128)(2,1)}, bf16[4096,512]{1,0:T(8,128)(2,1)S(1)}, u32[]{:S(2)}) copy-start(bf16[4096,512]{1,0:T(8,128)(2,1)S(1)} %get-tuple-element.7) | copy-start | bytes 12582916
  304.6 14.6 %copy-start.2 = (bf16[4096,1,96]{0,2,1:T(8,128)(2,1)S(1)}, bf16[4096,1,96]{0,2,1:T(8,128)(2,1)}, u32[]{:S(2)}) copy-start(bf16[4096,1,96]{0,2,1:T(8,128)(2,1)} %slice.129) | copy-start | bytes 2359300
  304.6 14.6 %copy-start.19 = (bf16[4096,1,16]{0,2,1:T(8,128)(2,1)S(1)}, bf16[4096,1,16]{0,2,1:T(8,128)(2,1)}, u32[]{:S(2)}) copy-start(bf16[4096,1,16]{0,2,1:T(8,128)(2,1)} %get-tuple-element.11) | copy-start | bytes 393220
  304.6 14.6 %copy-start.20 = (bf16[4096,1,16]{0,2,1:T(8,128)(2,1)S(1)}, bf16[4096,1,16]{0,2,1:T(8,128)(2,1)}, u32[]{:S(2)}) copy-start(bf16[4096,1,16]{0,2,1:T(8,128)(2,1)} %get-tuple-element.12) | copy-start | bytes 393220
  304.6 14.7 %copy-start.3 = (bf16[4096,1,96]{0,2,1:T(8,128)(2,1)S(1)}, bf16[4096,1,96]{0,2,1:T(8,128)(2,1)}, u32[]{:S(2)}) copy-start(bf16[4096,1,96]{0,2,1:T(8,128)(2,1)} %slice.128) | copy-start | bytes 2359300
  304.6 14.7 %copy-start.17 = (bf16[4096,1,16]{0,2,1:T(8,128)(2,1)S(1)}, bf16[4096,1,16]{0,2,1:T(8,128)(2,1)}, u32[]{:S(2)}) copy-start(bf16[4096,1,16]{0,2,1:T(8,128)(2,1)} %get-tuple-element.19) | copy-start | bytes 393220
  304.6 14.7 %copy-start.18 = (bf16[4096,1,16]{0,2,1:T(8,128)(2,1)S(1)}, bf16[4096,1,16]{0,2,1:T(8,128)(2,1)}, u32[]{:S(2)}) copy-start(bf16[4096,1,16]{0,2,1:T(8,128)(2,1)} %get-tuple-element.20) | copy-start | bytes 393220
  343.8 14.6 %copy-start.35 = (bf16[4096,512]{1,0:T(8,128)(2,1)S(1)}, bf16[4096,512]{1,0:T(8,128)(2,1)}, u32[]{:S(2)}) copy-start(bf16[4096,512]{1,0:T(8,128)(2,1)} %copy-done.34) | copy-start | bytes 12582916
  371.8 18.6 %copy-start.26 = (f32[4096]{0:T(1024)S(1)}, f32[4096]{0:T(1024)}, u32[]{:S(2)}) copy-start(f32[4096]{0:T(1024)} %copy-done.25) | copy-start | bytes 49156
  371.8 18.6 %copy-start.28 = (f32[4096]{0:T(1024)S(1)}, f32[4096]{0:T(1024)}, u32[]{:S(2)}) copy-start(f32[4096]{0:T(1024)} %copy-done.27) | copy-start | bytes 49156
  390.5 150.5 %copy-start.21 = (f32[4096]{0:T(1024)S(1)}, f32[4096]{0:T(1024)}, u32[]{:S(2)}) copy-start(f32[4096]{0:T(1024)} %param.10) | copy-start | bytes 49156
  390.5 150.5 %copy-start.22 = (f32[4096]{0:T(1024)S(1)}, f32[4096]{0:T(1024)}, u32[]{:S(2)}) copy-start(f32[4096]{0:T(1024)} %param.11) | copy-start | bytes 49156
  390.5 150.5 %copy-start.24 = (f32[2048]{0:T(1024)S(1)}, f32[2048]{0:T(1024)}, u32[]{:S(2)}) copy-start(f32[2048]{0:T(1024)} %copy-done.23) | copy-start | bytes 24580
  (5 other events, 41.2 us)
Sparse Core Ops, SparseCore 0:
  343.9 196.9 all-reduce.1
where the time goes:
time: 599 us; the launch traced here: 591 us
  matrix products  313 us (52%)
  other arithmetic  140 us (23%)
  waiting for transfers between devices  117 us (20%)
  between operations  15 us (3%)
    psum x1, waiting for transfers between devices, device_step(): lax.psum(part_sum.astype(jnp.bfloat16), 'model').astype(jnp.float32)  117 us
    convert_element_type x1, other arithmetic, attention_pair(): (attn_probs * (d_probs - row_delta) * att_scale).astype(jnp.bfloat16)  53.6 us
    dot_general x1, matrix products, attention_pair(): jnp.einsum('...qhd,...khd->...hqk', d_attn, values, preferred_element_typ...  49.3 us
    dot_general x1, matrix products, device_step(): jnp.einsum('thd,te->hde', attn_out, grad_y, preferred_element_type=jnp.fl...  33.8 us
    dot_general x1, matrix products, device_step(): lax.dot_general(grad_y, w_down, CONTRACT_COLS, preferred_element_type=jnp...  33.1 us
    dot_general x1, matrix products, attention_pair(): jnp.einsum('...hqk,...qhd->...khd', probs_bf, d_attn, preferred_element_t...  28.8 us
    convert_element_type x1, other arithmetic, ln_backward(): return (grad_y.astype(jnp.float32) + grad_in).astype(jnp.bfloat16)  26.3 us
    dot_general x1, matrix products, attention_pair(): jnp.einsum('...qhd,...khd->...hqk', q_rot, k_rot, preferred_element_type=...  24.2 us
  transfers between devices with their start and end apart: 1, of which 1 were waited for; matrix products, arithmetic and copies ran while one was open for 14% of the time, Pallas kernels for 0%

commit v1 on v0

v1 whole, which is shorter than its diff:
```python
import functools

import jax
import jax.numpy as jnp
from jax import lax
from jax.experimental import pallas as pl
from jax.experimental.pallas import tpu as pltpu
from jax.sharding import PartitionSpec as P

BF = jnp.bfloat16
F32 = jnp.float32
BLK = 512
MLP_ROWS = 256
WG_ROWS = 512
LN_ROWS = 256
CHUNK_BLOCKS = (1, 2, 2, 2, 1)
VMEM_LIMIT = 64 * 1000 * 1024


def dot_nn(a, b):
    return lax.dot_general(a, b, (((1,), (0,)), ((), ())), preferred_element_type=F32)


def dot_nt(a, b):
    return lax.dot_general(a, b, (((1,), (1,)), ((), ())), preferred_element_type=F32)


def dot_tn(a, b):
    return lax.dot_general(a, b, (((0,), (0,)), ((), ())), preferred_element_type=F32)


def column(row):
    return jnp.broadcast_to(row, (128, row.shape[1])).T[:, :1]


def rotate_t(x, cos_t, sin_t):
    half = cos_t.shape[0]
    a, b = x[:half], x[half:2 * half]
    return jnp.concatenate([a * cos_t - b * sin_t, b * cos_t + a * sin_t, x[2 * half:]], axis=0)


def whole(shape, index=None):
    index = index or (0,) * len(shape)
    return pl.BlockSpec(shape, lambda i: index, pipeline_mode=pl.Buffered(1))


ANY = pl.BlockSpec(memory_space=pl.ANY)


def params():
    return pltpu.CompilerParams(dimension_semantics=("arbitrary",), vmem_limit_bytes=VMEM_LIMIT)


def cost(flops, nbytes):
    return pl.CostEstimate(flops=int(flops), bytes_accessed=int(nbytes), transcendentals=0)


def qkv_kernel(x_ref, mean_ref, rstd_ref, g_ref, w_ref, cos_ref, sin_ref, n_ref, q_ref, k_ref, v_ref, kt_ref, vt_ref):
    hd = q_ref.shape[1]
    xh = (x_ref[...].astype(F32) - column(mean_ref[...])) * column(rstd_ref[...])
    n = (xh * g_ref[...].astype(F32)).astype(BF)
    n_ref[...] = n
    proj = dot_nn(n, w_ref[...])
    cos_t, sin_t = cos_ref[...], sin_ref[...]
    q_ref[...] = rotate_t(proj[:, :hd].T, cos_t, sin_t).T.astype(BF)
    kt = rotate_t(proj[:, hd:2 * hd].T, cos_t, sin_t)
    kt_ref[...] = kt.astype(BF)
    k_ref[...] = kt.T.astype(BF)
    v = proj[:, 2 * hd:]
    v_ref[...] = v.astype(BF)
    vt_ref[...] = v.T.astype(BF)


def qkv_call(x, mean, rstd, g, w, cos_t, sin_t):
    t, d = x.shape
    cols = w.shape[1]
    hd = cols // 3
    half = cos_t.shape[0]
    rows = lambda width: pl.BlockSpec((BLK, width), lambda i: (i, 0))
    lanes = lambda height: pl.BlockSpec((height, BLK), lambda i: (0, i))
    sd = lambda *s: jax.ShapeDtypeStruct(s, BF)
    return pl.pallas_call(
        qkv_kernel,
        grid=(t // BLK,),
        in_specs=[rows(d), lanes(1), lanes(1), whole((1, d)), whole((d, cols)), lanes(half), lanes(half)],
        out_specs=[rows(d), rows(hd), rows(hd), rows(hd), lanes(hd), lanes(hd)],
        out_shape=[sd(t, d), sd(t, hd), sd(t, hd), sd(t, hd), sd(hd, t), sd(hd, t)],
        compiler_params=params(),
        cost_estimate=cost(2 * t * d * cols, 4 * t * d),
        name="ln_qkv",
    )(x, mean, rstd, g, w, cos_t, sin_t)


def attn_kernel(top, n_steps, left, has_in, head_dim, *refs):
    n_in = 9 + (4 if has_in else 0)
    ins, rest = refs[:n_in], refs[n_in:]
    q_ref, k_ref, v_ref, kt_ref, vt_ref, dy_ref, wo_ref, cos_ref, sin_ref = ins[:9]
    o_ref, dqkv_ref = rest[:2]
    rest = rest[2:]
    if left:
        dk_out, dv_out = rest[:2]
        rest = rest[2:]
    s_ref, dp_ref, dk_acc, dv_acc, ot_acc, dqt_acc = rest
    step = pl.program_id(0)
    i = top - step
    scale = head_dim ** -0.5
    log2e = 1.4426950408889634

    @pl.when(step == 0)
    def _():
        if has_in:
            dk_acc[...] = ins[9][...]
            dv_acc[...] = ins[10][...]
        else:
            dk_acc[...] = jnp.zeros_like(dk_acc)
            dv_acc[...] = jnp.zeros_like(dv_acc)

    q = q_ref[...]
    d_out = dot_nt(dy_ref[...], wo_ref[0]).astype(BF)
    ot_acc[...] = jnp.zeros_like(ot_acc)
    dqt_acc[...] = jnp.zeros_like(dqt_acc)

    def at(j):
        return pl.ds(pl.multiple_of(j * BLK, BLK), BLK)

    s = dot_nt(k_ref[at(i), :], q) * (scale * log2e)
    key = lax.broadcasted_iota(jnp.int32, (BLK, BLK), 0)
    query = lax.broadcasted_iota(jnp.int32, (BLK, BLK), 1)
    s = jnp.where(key <= query, s, -1e30)
    s_ref[at(i), :] = s
    m = jnp.max(s, axis=0, keepdims=True)
    l = jnp.sum(jnp.exp2(s - m), axis=0, keepdims=True)

    def scores(j, carry):
        m, l = carry
        s = dot_nt(k_ref[at(j), :], q) * (scale * log2e)
        s_ref[at(j), :] = s
        m_new = jnp.maximum(m, jnp.max(s, axis=0, keepdims=True))
        l = l * jnp.exp2(m - m_new) + jnp.sum(jnp.exp2(s - m_new), axis=0, keepdims=True)
        return m_new, l

    m, l = lax.fori_loop(0, i, scores, (m, l))
    m = m + jnp.log2(l)

    def probs(j, delta):
        p = jnp.exp2(s_ref[at(j), :] - m)
        pb = p.astype(BF)
        dp = dot_nt(v_ref[at(j), :], d_out)
        s_ref[at(j), :] = p
        dp_ref[at(j), :] = dp
        dv_acc[at(j), :] += dot_nn(pb, d_out)
        ot_acc[...] += dot_nn(vt_ref[:, at(j)], pb)
        return delta + jnp.sum(p * dp, axis=0, keepdims=True)

    delta = lax.fori_loop(0, i + 1, probs, jnp.zeros((1, BLK), F32))

    def grads(j, carry):
        ds = (s_ref[at(j), :] * (dp_ref[at(j), :] - delta) * scale).astype(BF)
        dk_acc[at(j), :] += dot_nn(ds, q)
        dqt_acc[...] += dot_nn(kt_ref[:, at(j)], ds)
        return carry

    lax.fori_loop(0, i + 1, grads, 0)

    cos_t, sin_t = cos_ref[...], sin_ref[...]
    o_ref[...] = ot_acc[...].T.astype(BF)
    dqkv_ref[:, :head_dim] = rotate_t(dqt_acc[...], cos_t, -sin_t).T.astype(BF)
    dqkv_ref[:, head_dim:2 * head_dim] = rotate_t(dk_acc[at(i), :].T, cos_t, -sin_t).T.astype(BF)
    dqkv_ref[:, 2 * head_dim:] = dv_acc[at(i), :].astype(BF)

    if left:
        @pl.when(step == n_steps - 1)
        def _():
            dk_out[...] = dk_acc[:left, :]
            dv_out[...] = dv_acc[:left, :]


def attn_call(block0, block1, qkv, dy, wo, cos_t, sin_t, carried):
    q, k, v, kt, vt = qkv
    t, hd = q.shape
    d = dy.shape[1]
    half = cos_t.shape[0]
    end, left = block1 * BLK, block0 * BLK
    n_steps = block1 - block0
    top = block1 - 1
    rows = lambda width: pl.BlockSpec((BLK, width), lambda s: (top - s, 0))
    lanes = lambda height: pl.BlockSpec((height, BLK), lambda s: (0, top - s))
    in_specs = [rows(hd), whole((end, hd)), whole((end, hd)), whole((hd, end)), whole((hd, end)), rows(d), whole((1, hd, d)), lanes(half), lanes(half)]
    args = [q, k, v, kt, vt, dy, wo, cos_t, sin_t]
    aliases = {}
    if carried is not None:
        in_specs += [whole((end, hd)), whole((end, hd)), ANY, ANY]
        args += list(carried)
        aliases = {11: 0, 12: 1}
    out_specs = [rows(hd), rows(3 * hd)]
    out_shape = [jax.ShapeDtypeStruct((t, hd), BF), jax.ShapeDtypeStruct((t, 3 * hd), BF)]
    if left:
        out_specs += [whole((left, hd)), whole((left, hd))]
        out_shape += [jax.ShapeDtypeStruct((left, hd), F32)] * 2
    tiles = sum(b + 1 for b in range(block0, block1))
    return pl.pallas_call(
        functools.partial(attn_kernel, top, n_steps, left, carried is not None, hd),
        grid=(n_steps,),
        in_specs=in_specs,
        out_specs=out_specs,
        out_shape=out_shape,
        scratch_shapes=[
            pltpu.VMEM((end, BLK), F32), pltpu.VMEM((end, BLK), F32),
            pltpu.VMEM((end, hd), F32), pltpu.VMEM((end, hd), F32),
            pltpu.VMEM((hd, BLK), F32), pltpu.VMEM((hd, BLK), F32),
        ],
        input_output_aliases=aliases,
        compiler_params=params(),
        cost_estimate=cost(12 * tiles * BLK * BLK * hd * 2, 8 * end * hd),
        name=f"attention_{block0}",
    )(*args)


def mlp_kernel(n_ref, dy_ref, dqkv_ref, w1_ref, w2_ref, wqkv_ref, *refs):
    part_ref, g_ref, da_ref = refs[-3:]
    w1 = w1_ref[...]
    a = dot_nn(n_ref[...], w1)
    dg = dot_nt(dy_ref[...], w2_ref[...])
    cdf = 0.5 * (1.0 + lax.erf(a * 0.7071067811865476))
    g_ref[...] = (a * cdf).astype(BF)
    pdf = jnp.exp(a * a * -0.5) * 0.3989422804014327
    da = (dg * (cdf + a * pdf)).astype(BF)
    da_ref[...] = da
    part_ref[...] = (dot_nt(da, w1) + dot_nt(dqkv_ref[...], wqkv_ref[...])).astype(BF)


def mlp_call(block0, block1, n, dy, dqkv, w1, w2, wqkv, carried):
    t, d = n.shape
    ff = w1.shape[1]
    cols = wqkv.shape[1]
    per = BLK // MLP_ROWS
    first, steps = block0 * per, (block1 - block0) * per
    rows = lambda width: pl.BlockSpec((MLP_ROWS, width), lambda s: (first + s, 0))
    in_specs = [rows(d), rows(d), rows(cols), whole((d, ff)), whole((ff, d)), whole((d, cols))]
    args = [n, dy, dqkv, w1, w2, wqkv]
    aliases = {}
    if carried is not None:
        in_specs += [ANY, ANY]
        args += list(carried)
        aliases = {6: 1, 7: 2}
    size = (block1 - block0) * BLK
    return pl.pallas_call(
        mlp_kernel,
        grid=(steps,),
        in_specs=in_specs,
        out_specs=[pl.BlockSpec((MLP_ROWS, d), lambda s: (s, 0)), rows(ff), rows(ff)],
        out_shape=[jax.ShapeDtypeStruct((size, d), BF), jax.ShapeDtypeStruct((t, ff), BF), jax.ShapeDtypeStruct((t, ff), BF)],
        input_output_aliases=aliases,
        compiler_params=params(),
        cost_estimate=cost(2 * size * d * (3 * ff + cols), 6 * size * d),
        name=f"mlp_{block0}",
    )(*args)


def wgrad_down_kernel(dy_ref, g_ref, o_ref, w2_out, wo_out, acc2, acco):
    step = pl.program_id(0)

    @pl.when(step == 0)
    def _():
        acc2[...] = jnp.zeros_like(acc2)
        acco[...] = jnp.zeros_like(acco)

    dy = dy_ref[...]
    acc2[...] += dot_tn(g_ref[...], dy)
    acco[...] += dot_tn(o_ref[...], dy)

    @pl.when(step == pl.num_programs(0) - 1)
    def _():
        w2_out[...] = acc2[...].astype(BF)
        wo_out[0] = acco[...].astype(BF)


def wgrad_up_kernel(n_ref, da_ref, dqkv_ref, w1_out, wqkv_out, acc1, accq):
    step = pl.program_id(0)

    @pl.when(step == 0)
    def _():
        acc1[...] = jnp.zeros_like(acc1)
        accq[...] = jnp.zeros_like(accq)

    def part(c, carry):
        at = pl.ds(pl.multiple_of(c * 512, 512), 512)
        n = n_ref[:, at]
        acc1[at, :] += dot_tn(n, da_ref[...])
        accq[at, :] += dot_tn(n, dqkv_ref[...])
        return carry

    lax.fori_loop(0, acc1.shape[0] // 512, part, 0)

    @pl.when(step == pl.num_programs(0) - 1)
    def _():
        w1_out[...] = acc1[...].astype(BF)
        wqkv_out[...] = accq[...].astype(BF)


def wgrad_call(kernel, big, left, right, shapes, name):
    t = big.shape[0]
    rows = lambda a: pl.BlockSpec((WG_ROWS, a.shape[1]), lambda i: (i, 0))
    flat = [s[-2:] for s in shapes]
    return pl.pallas_call(
        kernel,
        grid=(t // WG_ROWS,),
        in_specs=[rows(big), rows(left), rows(right)],
        out_specs=[whole(s) for s in shapes],
        out_shape=[jax.ShapeDtypeStruct(s, BF) for s in shapes],
        scratch_shapes=[pltpu.VMEM(s, F32) for s in flat],
        compiler_params=params(),
        cost_estimate=cost(2 * t * big.shape[1] * (left.shape[1] + right.shape[1]), 4 * t * big.shape[1]),
        name=name,
    )(big, left, right)


def ln_kernel(dn_ref, x_ref, dy_ref, mean_ref, rstd_ref, g_ref, *refs):
    out_ref = refs[-1]
    rstd = column(rstd_ref[...])
    xh = (x_ref[...].astype(F32) - column(mean_ref[...])) * rstd
    d = dn_ref[...].astype(F32) * g_ref[...].astype(F32)
    inv = 1.0 / d.shape[1]
    mean_d = jnp.sum(d, axis=1, keepdims=True) * inv
    mean_dx = jnp.sum(d * xh, axis=1, keepdims=True) * inv
    out_ref[...] = (dy_ref[...].astype(F32) + rstd * (d - mean_d - xh * mean_dx)).astype(BF)


def ln_call(block0, block1, dn, x, dy, mean, rstd, g, carried, after):
    t, d = x.shape
    per = BLK // LN_ROWS
    first, steps = block0 * per, (block1 - block0) * per
    rows = pl.BlockSpec((LN_ROWS, d), lambda s: (first + s, 0))
    lanes = pl.BlockSpec((1, LN_ROWS), lambda s: (0, first + s))
    in_specs = [pl.BlockSpec((LN_ROWS, d), lambda s: (s, 0)), rows, rows, lanes, lanes, whole((1, d))]
    args = [dn, x, dy, mean, rstd, g]
    aliases = {}
    if carried is not None:
        in_specs += [ANY]
        args += [carried]
        aliases = {6: 0}
    in_specs += [ANY] * len(after)
    args += list(after)
    return pl.pallas_call(
        ln_kernel,
        grid=(steps,),
        in_specs=in_specs,
        out_specs=rows,
        out_shape=jax.ShapeDtypeStruct((t, d), BF),
        input_output_aliases=aliases,
        compiler_params=params(),
        cost_estimate=cost(20 * dn.shape[0] * d, 8 * dn.shape[0] * d),
        name=f"ln_backward_{block0}",
    )(*args)


def solution(mesh):
    def device_step(resid_x, ln_mean, ln_rstd, ln_gain, grad_y, w_qkv, w_out, w_up, w_down):
        n_model = mesh.shape["model"]
        tokens, d = resid_x.shape
        hd = w_out.shape[1]
        rot = hd // 4
        positions = jnp.arange(tokens, dtype=F32)[None, :]
        inv_freq = jnp.power(10000.0, -2.0 * jnp.arange(rot // 2, dtype=F32) / rot)
        angles = positions * inv_freq[:, None]
        cos_t, sin_t = jnp.cos(angles), jnp.sin(angles)
        mean, rstd, gain = ln_mean[None, :], ln_rstd[None, :], ln_gain[None, :]

        normed, *qkv = qkv_call(resid_x, mean, rstd, gain, w_qkv, cos_t, sin_t)

        bounds = []
        top = tokens // BLK
        for size in CHUNK_BLOCKS:
            bounds.append((top - size, top))
            top -= size
        assert top == 0
        carried, mlp_carried, sums = None, None, []
        for block0, block1 in bounds:
            o, dqkv, *acc = attn_call(block0, block1, qkv, grad_y, w_out, cos_t, sin_t, carried)
            carried = (*acc, o, dqkv)
            part, act, d_pre = mlp_call(block0, block1, normed, grad_y, dqkv, w_up, w_down, w_qkv, mlp_carried)
            mlp_carried = (act, d_pre)
            sums.append(lax.psum(part, "model", axis_index_groups=[[(r + len(sums)) % n_model for r in range(n_model)]]))

        ff = w_up.shape[1]
        grad_w_down, grad_w_out = wgrad_call(wgrad_down_kernel, grad_y, act, o, [(ff, d), (1, hd, d)], "wgrad_down")
        grad_w_up, grad_w_qkv = wgrad_call(wgrad_up_kernel, normed, d_pre, dqkv, [(d, ff), (d, 3 * hd)], "wgrad_up")

        grad_x = None
        after = [grad_w_down, grad_w_up]
        for (block0, block1), dn in zip(bounds, sums):
            grad_x = ln_call(block0, block1, dn, resid_x, grad_y, mean, rstd, gain, grad_x, after)
            after = []
        return grad_x, grad_w_qkv, grad_w_out, grad_w_up, grad_w_down

    in_specs = (P("data", None), P("data"), P("data"), P(None), P("data", None), P(None, "model"), P("model", None, None), P(None, "model"), P("model", None))
    out_specs = (P("data", None), P("data", "model"), P(("data", "model"), None, None), P("data", "model"), P(("data", "model"), None))
    return jax.shard_map(device_step, mesh=mesh, in_specs=in_specs, out_specs=out_specs, check_vma=False)
```

time: 599 us -> 648 us (1.082); the launches traced: 591 us -> 648 us
  matrix products: 313 us -> 0 us
  waiting for transfers between devices: 117 us -> 382 us
  Pallas kernels: 0 us -> 248 us
  other arithmetic: 140 us -> 1.86 us
    dot_general x15 -> x0, matrix products: 313 us -> none  [the longest x1 49.3 us: attention_pair(): jnp.einsum('...qhd,...khd->...hqk', d_attn, values, preferred_element_typ...]
    psum x1 -> x5, waiting for transfers between devices: 117 us -> 382 us  [device_step(): lax.psum(part, 'model', axis_index_groups=[[(r + len(sums)) % n_model for...]
    pallas_call x0 -> x18, Pallas kernels: none -> 248 us  [the longest x5 81.4 us: attn_call(): pl.pallas_call(functools.partial(attn_kernel, top, n_steps, left, carried...]
    convert_element_type x4 -> x0, other arithmetic: 96.7 us -> none  [the longest x1 53.6 us: attention_pair(): (attn_probs * (d_probs - row_delta) * att_scale).astype(jnp.bfloat16)]
    reduce_sum x2 -> x0, other arithmetic: 38 us -> none  [the longest x1 21.8 us: attention_pair(): attn_probs = jax.nn.softmax(jnp.where(causal, scores, -1e+30), axis=-1)]
  transfers between devices with their start and end apart: 1 -> 5, of which waited for: 1 -> 4; matrix products, arithmetic and copies ran while one was open for 14% -> 0% of each run, Pallas kernels for 0% -> 30%
where the time goes in v1:
time: 648 us
  waiting for transfers between devices  382 us (59%)
  Pallas kernels  248 us (38%)
  between operations  13.8 us (2%)
    psum x5, waiting for transfers between devices, device_step(): lax.psum(part, 'model', axis_index_groups=[[(r + len(sums)) % n_model for...  382 us
    pallas_call x5, Pallas kernels, attn_call(): pl.pallas_call(functools.partial(attn_kernel, top, n_steps, left, carried...  81.4 us
    pallas_call x5, Pallas kernels, mlp_call(): pl.pallas_call(mlp_kernel, grid=(steps,), in_specs=in_specs, out_specs=[p...  61.7 us
    pallas_call x2, Pallas kernels, wgrad_call(): pl.pallas_call(kernel, grid=(t // WG_ROWS,), in_specs=[rows(big), rows(le...  45.8 us
    pallas_call x5, Pallas kernels, ln_call(): pl.pallas_call(ln_kernel, grid=(steps,), in_specs=in_specs, out_specs=row...  38.8 us
    pallas_call x1, Pallas kernels, qkv_call(): pl.pallas_call(qkv_kernel, grid=(t // BLK,), in_specs=[rows(d), lanes(1),...  20.3 us
  transfers between devices with their start and end apart: 5, of which 4 were waited for; matrix products, arithmetic and copies ran while one was open for 0% of the time, Pallas kernels for 30%

profile of v1, /device:TPU:21, one launch (start us, length us, event | category | flops | bytes accessed | tf_op | source)
XLA Modules:
  0.0 647.7 jit_solution(7781261460933683556)
XLA Ops:
  7.2 0.1 all-reduce.14.cloned.1.call-start
  7.3 1.3 broadcast_in_dim.13.g_ref
  8.5 1.8 fusion
  10.4 20.3 %ln_qkv.1 = (bf16[4096,2048]{1,0:T(8,128)(2,1)}, bf16[4096,128]{1,0:T(8,128)(2,1)}, bf16[4096,128]{1,0:T(8,128)(2,1)}, bf16[4096,128]{1,0:T(8,128)(2,1)}, bf16[1...) custom-call(bf16[4096,2048]{1,0:T(8,128)(2,1)} %x_ref.11, f32[1,4096]{1,0:T(1,128)} %bitcast.2, f32[1,4096]{1,0:T(1,128)} %bitcast.8, ...), custom_call_target="tpu_custom_call" | custom-call | flops 6442450944 | bytes 33554432 | tf_op jit(solution)/shard_map/ln_qkv/pallas_call | solution.py:82
  30.7 17.1 %attention_7.1 = (bf16[4096,128]{1,0:T(8,128)(2,1)}, bf16[4096,384]{1,0:T(8,128)(2,1)}, f32[3584,128]{1,0:T(8,128)}, f32[3584,128]{1,0:T(8,128)}) custom-call(bf16[4096,128]{1,0:T(8,128)(2,1)} %get-tuple-element.49.refs_0_, bf16[4096,128]{1,0:T(8,128)(2,1)} %get-tuple-element.50.refs_1_, bf16[4096,128]{1,0:T(8,128)(2,1)} %get-tuple-element.51.refs_2_, ...), custom_call_target="tpu_custom_call" | custom-call | flops 6442450944 | bytes 4194304 | tf_op jit(solution)/shard_map/attention_7/pallas_call | solution.py:201
  47.8 9.7 %mlp_7.1 = (bf16[512,2048]{1,0:T(8,128)(2,1)}, bf16[4096,512]{1,0:T(8,128)(2,1)}, bf16[4096,512]{1,0:T(8,128)(2,1)}) custom-call(bf16[4096,2048]{1,0:T(8,128)(2,1)} %get-tuple-element.48.n_ref, bf16[4096,2048]{1,0:T(8,128)(2,1)} %dy_ref.21, bf16[4096,384]{1,0:T(8,128)(2,1)} %get-tuple-element.57.refs_12_.dqkv_ref, bf16[2048,512]{1,0:T(8,128)(2,1)} %w1_ref.9, ...), custom_call_target="tpu_custom_call" | custom-call | flops 4026531840 | bytes 6291456 | tf_op jit(solution)/shard_map/mlp_7/pallas_call | solution.py:247
  57.5 0.1 all-reduce.14.cloned.1.call-update
  57.6 0.1 all-reduce.12.cloned.1.call-start
  57.6 26.4 %attention_5.1 = (bf16[4096,128]{1,0:T(8,128)(2,1)}, bf16[4096,384]{1,0:T(8,128)(2,1)}, f32[2560,128]{1,0:T(8,128)}, f32[2560,128]{1,0:T(8,128)}) custom-call(bf16[4096,128]{1,0:T(8,128)(2,1)} %get-tuple-element.49.refs_0_, bf16[4096,128]{1,0:T(8,128)(2,1)} %get-tuple-element.50.refs_1_, ...), custom_call_target="tpu_custom_call", output_to_operand_aliasing={{0}: (11, {}), {1}: (12, {})} | custom-call | flops 10468982784 | bytes 3670016 | tf_op jit(solution)/shard_map/attention_5/pallas_call | solution.py:201
  84.0 14.2 %mlp_5.1 = (bf16[1024,2048]{1,0:T(8,128)(2,1)}, bf16[4096,512]{1,0:T(8,128)(2,1)}, bf16[4096,512]{1,0:T(8,128)(2,1)}) custom-call(bf16[4096,2048]{1,0:T(8,128)(2,1)} %get-tuple-element.48.n_ref, bf16[4096,2048]{1,0:T(8,128)(2,1)} %dy_ref.21, bf16[4096,384]{1,0:T(8,128)(2,1)} %get-tuple-element.61.refs_12_.dqkv_ref, ...), custom_call_target="tpu_custom_call", output_to_operand_aliasing={{1}: (6, {}), {2}: (7, {})} | custom-call | flops 8053063680 | bytes 12582912 | tf_op jit(solution)/shard_map/mlp_5/pallas_call | solution.py:247
  98.2 0.1 all-reduce.12.cloned.1.call-update
  98.3 0.2 all-reduce.10.cloned.1.call-start
  98.5 19.6 %attention_3.1 = (bf16[4096,128]{1,0:T(8,128)(2,1)}, bf16[4096,384]{1,0:T(8,128)(2,1)}, f32[1536,128]{1,0:T(8,128)}, f32[1536,128]{1,0:T(8,128)}) custom-call(bf16[4096,128]{1,0:T(8,128)(2,1)} %get-tuple-element.49.refs_0_, bf16[4096,128]{1,0:T(8,128)(2,1)} %get-tuple-element.50.refs_1_, ...), custom_call_target="tpu_custom_call", output_to_operand_aliasing={{0}: (11, {}), {1}: (12, {})} | custom-call | flops 7247757312 | bytes 2621440 | tf_op jit(solution)/shard_map/attention_3/pallas_call | solution.py:201
  118.2 14.2 %mlp_3.1 = (bf16[1024,2048]{1,0:T(8,128)(2,1)}, bf16[4096,512]{1,0:T(8,128)(2,1)}, bf16[4096,512]{1,0:T(8,128)(2,1)}) custom-call(bf16[4096,2048]{1,0:T(8,128)(2,1)} %get-tuple-element.48.n_ref, bf16[4096,2048]{1,0:T(8,128)(2,1)} %dy_ref.21, bf16[4096,384]{1,0:T(8,128)(2,1)} %get-tuple-element.65.refs_12_.dqkv_ref, ...), custom_call_target="tpu_custom_call", output_to_operand_aliasing={{1}: (6, {}), {2}: (7, {})} | custom-call | flops 8053063680 | bytes 12582912 | tf_op jit(solution)/shard_map/mlp_3/pallas_call | solution.py:247
  132.4 0.1 all-reduce.10.cloned.1.call-update
  132.4 0.1 all-reduce.8.cloned.1.call-start
  132.5 13.0 %attention_1.1 = (bf16[4096,128]{1,0:T(8,128)(2,1)}, bf16[4096,384]{1,0:T(8,128)(2,1)}, f32[512,128]{1,0:T(8,128)}, f32[512,128]{1,0:T(8,128)}) custom-call(bf16[4096,128]{1,0:T(8,128)(2,1)} %get-tuple-element.49.refs_0_, bf16[4096,128]{1,0:T(8,128)(2,1)} %get-tuple-element.50.refs_1_, ...), custom_call_target="tpu_custom_call", output_to_operand_aliasing={{0}: (11, {}), {1}: (12, {})} | custom-call | flops 4026531840 | bytes 1572864 | tf_op jit(solution)/shard_map/attention_1/pallas_call | solution.py:201
  145.5 14.2 %mlp_1.1 = (bf16[1024,2048]{1,0:T(8,128)(2,1)}, bf16[4096,512]{1,0:T(8,128)(2,1)}, bf16[4096,512]{1,0:T(8,128)(2,1)}) custom-call(bf16[4096,2048]{1,0:T(8,128)(2,1)} %get-tuple-element.48.n_ref, bf16[4096,2048]{1,0:T(8,128)(2,1)} %dy_ref.21, bf16[4096,384]{1,0:T(8,128)(2,1)} %get-tuple-element.69.refs_12_.dqkv_ref, ...), custom_call_target="tpu_custom_call", output_to_operand_aliasing={{1}: (6, {}), {2}: (7, {})} | custom-call | flops 8053063680 | bytes 12582912 | tf_op jit(solution)/shard_map/mlp_1/pallas_call | solution.py:247
  159.7 0.1 all-reduce.6.cloned.1.call-start
  159.8 5.3 attention_0.1
  165.1 9.4 %mlp_0.1 = (bf16[512,2048]{1,0:T(8,128)(2,1)}, bf16[4096,512]{1,0:T(8,128)(2,1)}, bf16[4096,512]{1,0:T(8,128)(2,1)}) custom-call(bf16[4096,2048]{1,0:T(8,128)(2,1)} %get-tuple-element.48.n_ref, bf16[4096,2048]{1,0:T(8,128)(2,1)} %dy_ref.21, bf16[4096,384]{1,0:T(8,128)(2,1)} %get-tuple-element.70.dqkv_ref, ...), custom_call_target="tpu_custom_call", output_to_operand_aliasing={{1}: (6, {}), {2}: (7, {})} | custom-call | flops 4026531840 | bytes 6291456 | tf_op jit(solution)/shard_map/mlp_0/pallas_call | solution.py:247
  174.6 28.7 %wgrad_up.1 = (bf16[2048,512]{1,0:T(8,128)(2,1)}, bf16[2048,384]{1,0:T(8,128)(2,1)}) custom-call(bf16[4096,2048]{1,0:T(8,128)(2,1)} %get-tuple-element.48.n_ref, bf16[4096,512]{1,0:T(8,128)(2,1)} %get-tuple-element.87.da_ref, bf16[4096,384]{1,0:T(8,128)(2,1)} %get-tuple-element.70.dqkv_ref), custom_call_target="tpu_custom_call" | custom-call | flops 15032385536 | bytes 33554432 | tf_op jit(solution)/shard_map/wgrad_up/pallas_call | solution.py:305
  203.3 17.1 %wgrad_down.1 = (bf16[512,2048]{1,0:T(8,128)(2,1)}, bf16[1,128,2048]{2,1,0:T(8,128)(2,1)}) custom-call(bf16[4096,2048]{1,0:T(8,128)(2,1)} %dy_ref.21, bf16[4096,512]{1,0:T(8,128)(2,1)} %get-tuple-element.84.g_ref, bf16[4096,128]{1,0:T(8,128)(2,1)} %get-tuple-element.85.o_ref), custom_call_target="tpu_custom_call" | custom-call | flops 10737418240 | bytes 33554432 | tf_op jit(solution)/shard_map/wgrad_down/pallas_call | solution.py:305
  220.4 5.5 ln_backward_7.1.refs_0_
  225.8 62.8 %all-reduce.12.cloned.1.call-done.dn_ref = bf16[1024,2048]{1,0:T(8,128)(2,1)} async-done(((bf16[1024,2048]{1,0:T(8,128)(2,1)}), bf16[1024,2048]{1,0:T(8,128)(2,1)}) %all-reduce.12.cloned.1.call-update) | async-done | bytes 4194320 | tf_op jit(solution)/shard_map/psum | solution.py:383
  288.6 9.2 %ln_backward_5.1.refs_0_ = bf16[4096,2048]{1,0:T(8,128)(2,1)} custom-call(bf16[1024,2048]{1,0:T(8,128)(2,1)} %all-reduce.12.cloned.1.call-done.dn_ref, bf16[4096,2048]{1,0:T(8,128)(2,1)} %x_ref.11, bf16[4096,2048]{1,0:T(8,128)(2,1)} %dy_ref.21, f32[1,4096]{1,0:T(1,128)} %bitcast.4, f32[1,4096]{1,0:T(1,128)} %bitcast.10, ...), custom_call_target="tpu_custom_call", output_to_operand_aliasing={{}: (6, {})} | custom-call | flops 41943040 | bytes 16777216 | tf_op jit(solution)/shard_map/ln_backward_5/pallas_call | solution.py:344
  297.8 108.5 %all-reduce.10.cloned.1.call-done.dn_ref = bf16[1024,2048]{1,0:T(8,128)(2,1)} async-done(((bf16[1024,2048]{1,0:T(8,128)(2,1)}), bf16[1024,2048]{1,0:T(8,128)(2,1)}) %all-reduce.10.cloned.1.call-update) | async-done | bytes 4194320 | tf_op jit(solution)/shard_map/psum | solution.py:383
  406.3 9.2 %ln_backward_3.1.refs_0_ = bf16[4096,2048]{1,0:T(8,128)(2,1)} custom-call(bf16[1024,2048]{1,0:T(8,128)(2,1)} %all-reduce.10.cloned.1.call-done.dn_ref, bf16[4096,2048]{1,0:T(8,128)(2,1)} %x_ref.11, bf16[4096,2048]{1,0:T(8,128)(2,1)} %dy_ref.21, f32[1,4096]{1,0:T(1,128)} %bitcast.5, f32[1,4096]{1,0:T(1,128)} %bitcast.11, ...), custom_call_target="tpu_custom_call", output_to_operand_aliasing={{}: (6, {})} | custom-call | flops 41943040 | bytes 16777216 | tf_op jit(solution)/shard_map/ln_backward_3/pallas_call | solution.py:344
  415.5 108.4 %all-reduce.8.cloned.1.call-done.dn_ref = bf16[1024,2048]{1,0:T(8,128)(2,1)} async-done(((bf16[1024,2048]{1,0:T(8,128)(2,1)}), bf16[1024,2048]{1,0:T(8,128)(2,1)}) %all-reduce.8.cloned.1.call-update) | async-done | bytes 4194320 | tf_op jit(solution)/shard_map/psum | solution.py:383
  523.9 9.2 %ln_backward_1.1.refs_0_ = bf16[4096,2048]{1,0:T(8,128)(2,1)} custom-call(bf16[1024,2048]{1,0:T(8,128)(2,1)} %all-reduce.8.cloned.1.call-done.dn_ref, bf16[4096,2048]{1,0:T(8,128)(2,1)} %x_ref.11, bf16[4096,2048]{1,0:T(8,128)(2,1)} %dy_ref.21, f32[1,4096]{1,0:T(1,128)} %bitcast.6, f32[1,4096]{1,0:T(1,128)} %bitcast.12, ...), custom_call_target="tpu_custom_call", output_to_operand_aliasing={{}: (6, {})} | custom-call | flops 41943040 | bytes 16777216 | tf_op jit(solution)/shard_map/ln_backward_1/pallas_call | solution.py:344
  533.1 102.3 %all-reduce.6.cloned.1.call-done.dn_ref = bf16[512,2048]{1,0:T(8,128)(2,1)} async-done(((bf16[512,2048]{1,0:T(8,128)(2,1)}), bf16[512,2048]{1,0:T(8,128)(2,1)}) %all-reduce.6.cloned.1.call-update) | async-done | bytes 2097168 | tf_op jit(solution)/shard_map/psum | solution.py:383
  635.4 5.8 ln_backward_0.1
  (4 shorter events, 0.1 us)
Async XLA Ops:
  7.2 213.2 %all-reduce.14.cloned.1.call-start = ((), (), s32[]{:S(2)}) async-start(), calls=%async_computation.4 | async-start | bytes 4194304 | tf_op jit(solution)/shard_map/psum | solution.py:383
  57.6 231.1 %all-reduce.12.cloned.1.call-start = ((), (), s32[]{:S(2)}) async-start(), calls=%async_computation.3 | async-start | bytes 8388608 | tf_op jit(solution)/shard_map/psum | solution.py:383
  98.3 308.1 %all-reduce.10.cloned.1.call-start = ((), (), s32[]{:S(2)}) async-start(), calls=%async_computation.2 | async-start | bytes 8388608 | tf_op jit(solution)/shard_map/psum | solution.py:383
  132.4 391.5 %all-reduce.8.cloned.1.call-start = ((), (), s32[]{:S(2)}) async-start(), calls=%async_computation.1 | async-start | bytes 8388608 | tf_op jit(solution)/shard_map/psum | solution.py:383
  159.7 475.7 %all-reduce.6.cloned.1.call-start = ((), (), s32[]{:S(2)}) async-start(), calls=%async_computation | async-start | bytes 4194304 | tf_op jit(solution)/shard_map/psum | solution.py:383
Sparse Core Ops, SparseCore 0:
  57.7 113.3 all-reduce.13
  173.5 115.1 all-reduce.11
  291.0 115.2 all-reduce.9
  408.6 115.2 all-reduce.7
  526.1 109.2 all-reduce.5

commit v2 on v0

v2 whole, which is shorter than its diff:
```python
import functools

import jax
import jax.numpy as jnp
from jax import lax
from jax.experimental import pallas as pl
from jax.experimental.pallas import tpu as pltpu
from jax.sharding import PartitionSpec as P

BF = jnp.bfloat16
F32 = jnp.float32
BLK = 512
VMEM_LIMIT = 67043328
MESH = pl.DeviceIdType.MESH
CORES = 2
LOG2E = 1.4426950408889634


def dot_nn(a, b):
    return lax.dot_general(a, b, (((1,), (0,)), ((), ())), preferred_element_type=F32)


def dot_nt(a, b):
    return lax.dot_general(a, b, (((1,), (1,)), ((), ())), preferred_element_type=F32)


def dot_tn(a, b):
    return lax.dot_general(a, b, (((0,), (0,)), ((), ())), preferred_element_type=F32)


def column(row):
    return jnp.broadcast_to(row, (128, row.shape[1])).T[:, :1]


def rotate_t(x, cos_t, sin_t):
    half = cos_t.shape[0]
    a, b = x[:half], x[half:2 * half]
    return jnp.concatenate([a * cos_t - b * sin_t, b * cos_t + a * sin_t, x[2 * half:]], axis=0)


def whole(shape, index=None):
    index = index or (0,) * len(shape)
    return pl.BlockSpec(shape, lambda i: index, pipeline_mode=pl.Buffered(1))


ANY = pl.BlockSpec(memory_space=pl.ANY)


def params():
    return pltpu.CompilerParams(dimension_semantics=("arbitrary",), vmem_limit_bytes=VMEM_LIMIT)


def cost(flops, nbytes):
    return pl.CostEstimate(flops=int(flops), bytes_accessed=int(nbytes), transcendentals=0)


def qkv_kernel(x_ref, mean_ref, rstd_ref, g_ref, w_ref, cos_ref, sin_ref, n_ref, q_ref, k_ref, v_ref, kt_ref, vt_ref, stat_ref):
    hd = q_ref.shape[1]
    mean, rstd = column(mean_ref[...]), column(rstd_ref[...])
    lane = lax.broadcasted_iota(jnp.int32, stat_ref.shape, 1)
    stat_ref[...] = jnp.where(lane == 0, mean, rstd)
    xh = (x_ref[...].astype(F32) - mean) * rstd
    n = (xh * g_ref[...].astype(F32)).astype(BF)
    n_ref[...] = n
    proj = dot_nn(n, w_ref[...])
    cos_t, sin_t = cos_ref[...], sin_ref[...]
    q_ref[...] = rotate_t(proj[:, :hd].T, cos_t, sin_t).T.astype(BF)
    kt = rotate_t(proj[:, hd:2 * hd].T, cos_t, sin_t)
    kt_ref[...] = kt.astype(BF)
    k_ref[...] = kt.T.astype(BF)
    v = proj[:, 2 * hd:]
    v_ref[...] = v.astype(BF)
    vt_ref[...] = v.T.astype(BF)


def qkv_call(x, mean, rstd, g, w, cos_t, sin_t):
    t, d = x.shape
    cols = w.shape[1]
    hd = cols // 3
    half = cos_t.shape[0]
    rows = lambda width: pl.BlockSpec((BLK, width), lambda i: (i, 0))
    lanes = lambda height: pl.BlockSpec((height, BLK), lambda i: (0, i))
    sd = lambda *s: jax.ShapeDtypeStruct(s, BF)
    return pl.pallas_call(
        qkv_kernel,
        grid=(t // BLK,),
        in_specs=[rows(d), lanes(1), lanes(1), whole((1, d)), whole((d, cols)), lanes(half), lanes(half)],
        out_specs=[rows(d), rows(hd), rows(hd), rows(hd), lanes(hd), lanes(hd), rows(128)],
        out_shape=[sd(t, d), sd(t, hd), sd(t, hd), sd(t, hd), sd(hd, t), sd(hd, t), jax.ShapeDtypeStruct((t, 128), F32)],
        compiler_params=params(),
        cost_estimate=cost(2 * t * d * cols, 4 * t * d),
        name="ln_qkv",
    )(x, mean, rstd, g, w, cos_t, sin_t)


def layer_kernel(
    nb, nz, q_ref, k_ref, v_ref, kt_ref, vt_ref, dy_ref, n_ref, cos_ref, sin_ref, wo_ref, w1_ref, w2_ref, wqkv_ref, gain_ref, x_hbm, dy_hbm, stat_hbm,
    dx_hbm, gw1_hbm, gwqkv_hbm, gw2_hbm, gwo_hbm,
    s_ref, dk_acc, dv_acc, ot_acc, dqt_acc, d_out_ref, row_ref, o_ref, dqkv_ref, act_ref, da_ref, acc1, accq, acc2, acco,
    part, pair, stage, recv, shard, x_rows, dy_rows, stat_rows,
    pair_send, pair_recv, rs_send, rs_recv, ag_send, ag_recv, fin_send, fin_recv, load_sem, own_sem, out_sem, credit,
):
    hd = q_ref.shape[1]
    scale = hd ** -0.5
    half = BLK // CORES
    piece = half // nz
    hops = nz // 2
    g = pl.program_id(0)
    i = nb - 1 - g

    me = lax.axis_index("model")
    z, c = lax.div(me, CORES), lax.rem(me, CORES)
    sgn = 1 - 2 * c
    signs = (sgn, -sgn)
    wrap = lambda n: lax.rem(n + 2 * nz, nz)
    partner = z * CORES + (1 - c)
    toward = tuple(wrap(z + s) * CORES + c for s in signs)
    compute, reducing, gathering = g < nb, (g >= 1) & (g <= nb), g >= 2
    red_row = (nb - g) * BLK
    gat_row = (nb + 1 - g) * BLK

    def at(j):
        return pl.ds(pl.multiple_of(j * BLK, BLK), BLK)

    def rows(first, n):
        return pl.ds(pl.multiple_of(first, n), n)

    def remote(src, dst, send_sem, recv_sem, device):
        return pltpu.make_async_remote_copy(src_ref=src, dst_ref=dst, send_sem=send_sem, recv_sem=recv_sem, device_id={"model": device}, device_id_type=MESH)

    def pair_copy():
        return remote(part.at[rows((1 - c) * half, half), :], pair, pair_send, pair_recv, partner)

    def rs_copy(flow, s):
        return remote(stage.at[flow, s - 1], recv.at[flow, s - 1], rs_send.at[flow, s - 1], rs_recv.at[flow, s - 1], toward[flow])

    def mine(p):
        own = part[rows(c * half + p * piece, piece), :].astype(F32)
        return own + pair[rows(p * piece, piece), :].astype(F32)

    def rs_start(flow, s, prior):
        total = mine(wrap(z + signs[flow] * (hops + 1 - s)))
        if prior:
            total += recv[flow, s - 2].astype(F32)
        stage[flow, s - 1] = total.astype(BF)
        rs_copy(flow, s).start()

    def ag_rows(flow, back):
        return rows(gat_row + c * half + wrap(z - signs[flow] * back) * piece, piece)

    def ag_copy(flow, s):
        there = dx_hbm.at[ag_rows(flow, s - 1), :]
        return remote(shard if s == 1 else there, there, ag_send.at[flow, s - 1], ag_recv.at[flow, s - 1], toward[flow])

    def ag_wait(flow, s):
        ag_copy(flow, s).wait_send()
        here = dx_hbm.at[ag_rows(flow, s), :]
        remote(here, here, ag_send.at[flow, s - 1], ag_recv.at[flow, s - 1], toward[flow]).wait_recv()

    def fin_copy(core):
        block = dx_hbm.at[rows(gat_row + core * half, half), :]
        return remote(block, block, fin_send, fin_recv, partner)

    def own_rows(first):
        return rows(first + c * half + z * piece, piece)

    def loads():
        at_rows = own_rows(red_row)
        return [pltpu.make_async_copy(src.at[at_rows, :], dst, load_sem.at[n]) for n, (src, dst) in enumerate(((x_hbm, x_rows), (dy_hbm, dy_rows), (stat_hbm, stat_rows)))]

    def own_store(first):
        return pltpu.make_async_copy(shard, dx_hbm.at[own_rows(first), :], own_sem)

    def weight_stores():
        pairs = ((acc1, gw1_hbm), (accq, gwqkv_hbm), (acc2, gw2_hbm), (acco, gwo_hbm))
        return [pltpu.make_async_copy(src, dst, out_sem.at[n]) for n, (src, dst) in enumerate(pairs)]

    def tick(t):
        if t == 0:
            @pl.when(g >= 1)
            def _():
                pl.semaphore_wait(credit, 3)

            @pl.when(reducing)
            def _():
                pair_copy().start()
                for load in loads():
                    load.start()

            @pl.when(gathering)
            def _():
                for flow in range(2):
                    ag_copy(flow, 1).start()
        elif t % 2 == 1 and t <= 2 * hops - 1:
            s = (t + 1) // 2
            @pl.when(reducing)
            def _():
                if s == 1:
                    pair_copy().wait()
                else:
                    rs_copy(0, s - 1).wait()
                    if s > 2:
                        rs_copy(1, s - 1).wait()
                rs_start(0, s, s > 1)
                if s > 1:
                    rs_start(1, s, s > 2)
        elif t % 2 == 0 and t <= 2 * hops:
            s = t // 2
            @pl.when(gathering)
            def _():
                ag_wait(0, s)
                if s < hops:
                    ag_wait(1, s)
                if s < hops:
                    ag_copy(0, s + 1).start()
                    if s + 1 < hops:
                        ag_copy(1, s + 1).start()
                else:
                    own_store(gat_row).wait()
                    fin_copy(c).start()
        elif t == 2 * hops + 1:
            @pl.when(gathering)
            def _():
                fin_copy(c).wait_send()
                fin_copy(1 - c).wait_recv()

            @pl.when(reducing)
            def _():
                for flow in range(2):
                    rs_copy(flow, hops).wait()
                for load in loads():
                    load.wait()
                total = mine(z) + recv[0, hops - 1].astype(F32) + recv[1, hops - 1].astype(F32)
                d = total * gain_ref[...].astype(F32)
                rstd = stat_rows[:, 1:2]
                xh = (x_rows[...].astype(F32) - stat_rows[:, 0:1]) * rstd
                inv = 1.0 / d.shape[1]
                mean_d = jnp.sum(d, axis=1, keepdims=True) * inv
                mean_dx = jnp.sum(d * xh, axis=1, keepdims=True) * inv
                shard[...] = (dy_rows[...].astype(F32) + rstd * (d - mean_d - xh * mean_dx)).astype(BF)
                own_store(red_row).start()

            @pl.when(g <= nb)
            def _():
                for device in (partner, *toward):
                    pl.semaphore_signal(credit, inc=1, device_id={"model": device}, device_id_type=MESH)

    def scores():
        d_out_ref[...] = dot_nt(dy_ref[...], wo_ref[0]).astype(BF)
        ot_acc[...] = jnp.zeros_like(ot_acc)
        dqt_acc[...] = jnp.zeros_like(dqt_acc)
        q = q_ref[...]
        s = dot_nt(k_ref[at(i), :], q) * (scale * LOG2E)
        key = lax.broadcasted_iota(jnp.int32, (BLK, BLK), 0)
        query = lax.broadcasted_iota(jnp.int32, (BLK, BLK), 1)
        s = jnp.where(key <= query, s, -1e30)
        s_ref[at(i), :] = s
        m = jnp.max(s, axis=0, keepdims=True)
        l = jnp.sum(jnp.exp2(s - m), axis=0, keepdims=True)

        def step(j, carry):
            m, l = carry
            s = dot_nt(k_ref[at(j), :], q) * (scale * LOG2E)
            s_ref[at(j), :] = s
            m_new = jnp.maximum(m, jnp.max(s, axis=0, keepdims=True))
            l = l * jnp.exp2(m - m_new) + jnp.sum(jnp.exp2(s - m_new), axis=0, keepdims=True)
            return m_new, l

        m, l = lax.fori_loop(0, i, step, (m, l))
        row_ref[0:1, :] = m + jnp.log2(l)

    def probs(first, last):
        m = row_ref[0:1, :]

        def step(j, carry):
            pb = jnp.exp2(s_ref[at(j), :] - m).astype(BF)
            dv_acc[at(j), :] += dot_nn(pb, d_out_ref[...])
            ot_acc[...] += dot_nn(vt_ref[:, at(j)], pb)
            return carry

        lax.fori_loop(first, last, step, 0)

    def delta():
        row_ref[1:2, :] = jnp.sum(ot_acc[...] * d_out_ref[...].astype(F32).T, axis=0, keepdims=True)
        o_ref[...] = ot_acc[...].T.astype(BF)

    def grads(first, last):
        m, delta = row_ref[0:1, :], row_ref[1:2, :]

        def step(j, carry):
            dp = dot_nt(v_ref[at(j), :], d_out_ref[...])
            p = jnp.exp2(s_ref[at(j), :] - m)
            ds = (p * (dp - delta) * scale).astype(BF)
            dk_acc[at(j), :] += dot_nn(ds, q_ref[...])
            dqt_acc[...] += dot_nn(kt_ref[:, at(j)], ds)
            return carry

        lax.fori_loop(first, last, step, 0)

    def heads_done():
        cos_t, sin_t = cos_ref[...], sin_ref[...]
        dqkv_ref[:, :hd] = rotate_t(dqt_acc[...], cos_t, -sin_t).T.astype(BF)
        dqkv_ref[:, hd:2 * hd] = rotate_t(dk_acc[at(i), :].T, cos_t, -sin_t).T.astype(BF)
        dqkv_ref[:, 2 * hd:] = dv_acc[at(i), :].astype(BF)

    def mlp(h):
        r = slice(h * half, (h + 1) * half)
        a = dot_nn(n_ref[r, :], w1_ref[...])
        dg = dot_nt(dy_ref[r, :], w2_ref[...])
        cdf = 0.5 * (1.0 + lax.erf(a * 0.7071067811865476))
        act_ref[r, :] = (a * cdf).astype(BF)
        pdf = jnp.exp(a * a * -0.5) * 0.3989422804014327
        da_ref[r, :] = (dg * (cdf + a * pdf)).astype(BF)

    def wgrad_down():
        def step(n, carry):
            cols = rows(n * 512, 512)
            dy = dy_ref[:, cols]
            acc2[:, cols] += dot_tn(act_ref[...], dy)
            acco[:, cols] += dot_tn(o_ref[...], dy)
            return carry

        lax.fori_loop(0, acc2.shape[1] // 512, step, 0)

    def wgrad_up():
        def step(n, carry):
            down = rows(n * 512, 512)
            x = n_ref[:, down]
            acc1[down, :] += dot_tn(x, da_ref[...])
            accq[down, :] += dot_tn(x, dqkv_ref[...])
            return carry

        lax.fori_loop(0, acc1.shape[0] // 512, step, 0)

    def partial_dn():
        for h in range(CORES):
            r = slice(h * half, (h + 1) * half)
            part[r, :] = (dot_nt(da_ref[r, :], w1_ref[...]) + dot_nt(dqkv_ref[r, :], wqkv_ref[...])).astype(BF)

    @pl.when(g == 0)
    def _():
        barrier = pltpu.get_barrier_semaphore()
        for device in (partner, *toward):
            pl.semaphore_signal(barrier, inc=1, device_id={"model": device}, device_id_type=MESH)
        pl.semaphore_wait(barrier, 3)
        for ref in (dk_acc, dv_acc, acc1, accq, acc2, acco):
            ref[...] = jnp.zeros_like(ref)

    @pl.when(g == nb)
    def _():
        for store in weight_stores():
            store.start()

    middle = lax.div(i + 1, 2)
    pieces = (
        lambda: scores(),
        lambda: probs(0, middle),
        lambda: (probs(middle, i + 1), delta()),
        lambda: grads(0, middle),
        lambda: (grads(middle, i + 1), heads_done()),
        lambda: mlp(0),
        lambda: mlp(1),
        lambda: wgrad_down(),
        lambda: wgrad_up(),
        lambda: partial_dn(),
    )
    for t, work in enumerate(pieces):
        tick(t)

        @pl.when(compute)
        def _():
            work()

    @pl.when(g == nb + 1)
    def _():
        for store in weight_stores():
            store.wait()


def layer_call(mesh, qkv, stat, x, n, dy, wo, w1, w2, wqkv, gain, cos_t, sin_t):
    q, k, v, kt, vt = qkv
    t, hd = q.shape
    d = dy.shape[1]
    ff, cols = w1.shape[1], wqkv.shape[1]
    nb = t // BLK
    nz = mesh.shape["model"] // CORES
    rot = cos_t.shape[0]
    half = BLK // CORES
    piece = half // nz
    hops = nz // 2
    block = lambda g: jnp.maximum(nb - 1 - g, 0)
    rows = lambda width: pl.BlockSpec((BLK, width), lambda g: (block(g), 0))
    lanes = lambda height: pl.BlockSpec((height, BLK), lambda g: (0, block(g)))
    vm = pltpu.VMEM
    dma = pltpu.SemaphoreType.DMA
    return pl.pallas_call(
        functools.partial(layer_kernel, nb, nz),
        grid=(nb + 2,),
        in_specs=[rows(hd), whole((t, hd)), whole((t, hd)), whole((hd, t)), whole((hd, t)), rows(d), rows(d), lanes(rot), lanes(rot),
                  whole((1, hd, d)), whole((d, ff)), whole((ff, d)), whole((d, cols)), whole((1, d)), ANY, ANY, ANY],
        out_specs=[ANY] * 5,
        out_shape=[jax.ShapeDtypeStruct((t, d), BF)] + [jax.ShapeDtypeStruct(s, F32) for s in ((d, ff), (d, cols), (ff, d), (hd, d))],
        scratch_shapes=[
            vm((t, BLK), F32), vm((t, hd), F32), vm((t, hd), F32), vm((hd, BLK), F32), vm((hd, BLK), F32),
            vm((BLK, hd), BF), vm((8, BLK), F32), vm((BLK, hd), BF), vm((BLK, cols), BF), vm((BLK, ff), BF), vm((BLK, ff), BF),
            vm((d, ff), F32), vm((d, cols), F32), vm((ff, d), F32), vm((hd, d), F32),
            vm((BLK, d), BF), vm((half, d), BF), vm((2, hops, piece, d), BF), vm((2, hops, piece, d), BF), vm((piece, d), BF),
            vm((piece, d), BF), vm((piece, d), BF), vm((piece, 128), F32),
            dma, dma, dma((2, hops)), dma((2, hops)), dma((2, hops)), dma((2, hops)), dma, dma, dma((3,)), dma, dma((4,)),
            pltpu.SemaphoreType.REGULAR,
        ],
        compiler_params=pltpu.CompilerParams(dimension_semantics=("arbitrary",), vmem_limit_bytes=VMEM_LIMIT, collective_id=0, has_side_effects=True),
        cost_estimate=cost(2 * t * d * (5 * ff + 3 * cols), 12 * t * d),
        name="layer_backward",
    )(q, k, v, kt, vt, dy, n, cos_t, sin_t, wo, w1, w2, wqkv, gain, x, dy, stat)


def solution(mesh):
    def device_step(resid_x, ln_mean, ln_rstd, ln_gain, grad_y, w_qkv, w_out, w_up, w_down):
        tokens, d = resid_x.shape
        hd = w_out.shape[1]
        rot = hd // 4
        positions = jnp.arange(tokens, dtype=F32)[None, :]
        inv_freq = jnp.power(10000.0, -2.0 * jnp.arange(rot // 2, dtype=F32) / rot)
        angles = positions * inv_freq[:, None]
        cos_t, sin_t = jnp.cos(angles), jnp.sin(angles)
        mean, rstd, gain = ln_mean[None, :], ln_rstd[None, :], ln_gain[None, :]
        normed, *qkv, stat = qkv_call(resid_x, mean, rstd, gain, w_qkv, cos_t, sin_t)
        grad_x, gw_up, gw_qkv, gw_down, gw_out = layer_call(mesh, qkv, stat, resid_x, normed, grad_y, w_out, w_up, w_down, w_qkv, gain, cos_t, sin_t)
        return grad_x, gw_qkv.astype(BF), gw_out[None].astype(BF), gw_up.astype(BF), gw_down.astype(BF)

    in_specs = (P("data", None), P("data"), P("data"), P(None), P("data", None), P(None, "model"), P("model", None, None), P(None, "model"), P("model", None))
    out_specs = (P("data", None), P("data", "model"), P(("data", "model"), None, None), P("data", "model"), P(("data", "model"), None))
    return jax.shard_map(device_step, mesh=mesh, in_specs=in_specs, out_specs=out_specs, check_vma=False)
```

time: 599 us -> 320 us (0.53); the launches traced: 591 us -> 319 us
  matrix products: 313 us -> 0 us
  Pallas kernels: 0 us -> 295 us
  other arithmetic: 140 us -> 16 us
  waiting for transfers between devices: 117 us -> 0 us
  between operations: 15 us -> 0.65 us
    dot_general x15 -> x0, matrix products: 313 us -> none  [the longest x1 49.3 us: attention_pair(): jnp.einsum('...qhd,...khd->...hqk', d_attn, values, preferred_element_typ...]
    pallas_call x0 -> x2, Pallas kernels: none -> 295 us  [the longest x1 277 us: layer_call(): pl.pallas_call(functools.partial(layer_kernel, nb, nz), grid=(nb + 2,), i...]
    psum x1 -> x0, waiting for transfers between devices: 117 us -> none  [device_step(): lax.psum(part_sum.astype(jnp.bfloat16), 'model').astype(jnp.float32)]
    convert_element_type x4, other arithmetic: 96.7 us -> 14.2 us  [the longest x1 4.54 us: device_step(): gw_up.astype(BF)]
    reduce_sum x2 -> x0, other arithmetic: 38 us -> none  [the longest x1 21.8 us: attention_pair(): attn_probs = jax.nn.softmax(jnp.where(causal, scores, -1e+30), axis=-1)]
  transfers between devices with their start and end apart: 1 -> 0, of which waited for: 1 -> 0; matrix products, arithmetic and copies ran while one was open for 14% -> 0% of each run, Pallas kernels for 0% -> 0%
where the time goes in v2:
time: 320 us; the launch traced here: 319 us
  Pallas kernels  295 us (92%)
  other arithmetic  16 us (5%)
  local copies, waits for them, and re-layouts  7.45 us (2%)
    pallas_call x1, Pallas kernels, layer_call(): pl.pallas_call(functools.partial(layer_kernel, nb, nz), grid=(nb + 2,), i...  277 us
    pallas_call x1, Pallas kernels, qkv_call(): pl.pallas_call(qkv_kernel, grid=(t // BLK,), in_specs=[rows(d), lanes(1),...  17.6 us

profile of v2, /device:TPU:21, one launch (start us, length us, event | category | flops | bytes accessed | tf_op | source)
XLA Modules:
  0.0 319.2 jit_solution(8519246948128658205)
XLA Ops:
  0.6 1.3 broadcast_in_dim.14.g_ref.gain_ref
  1.9 1.8 fusion
  3.7 17.6 %ln_qkv.1 = (bf16[4096,2048]{1,0:T(8,128)(2,1)}, bf16[4096,128]{1,0:T(8,128)(2,1)}, bf16[4096,128]{1,0:T(8,128)(2,1)}, bf16[4096,128]{1,0:T(8,128)(2,1)}, bf16[1...) custom-call(bf16[4096,2048]{1,0:T(8,128)(2,1)} %x_hbm.1, f32[1,4096]{1,0:T(1,128)} %bitcast.4, ...), custom_call_target="tpu_custom_call" | custom-call | flops 6442450944 | bytes 33554432 | tf_op jit(solution)/shard_map/ln_qkv/pallas_call | solution.py:84
  21.4 277.4 %layer_backward.1 = (bf16[4096,2048]{1,0:T(8,128)(2,1)}, f32[2048,512]{1,0:T(8,128)}, f32[2048,384]{1,0:T(8,128)}, f32[512,2048]{1,0:T(8,128)}, f32[128,2048]{1,0:T(8,128)}) custom-call(bf16[4096,128]{1,0:T(8,128)(2,1)} %get-tuple-element.17.q_ref, bf16[4096,128]{1,0:T(8,128)(2,1)} %get-tuple-element.18.k_ref, bf16[4096,128]{1,0:T(8,128)(2,1)} %get-tuple-element.19.v_ref, ...), custom_call_target="tpu_custom_call" | custom-call | flops 62277025792 | bytes 100663296 | tf_op jit(solution)/shard_map/layer_backward/pallas_call | solution.py:396
  298.8 2.1 convert_bitcast_fusion
  300.9 0.0 copy-start
  300.9 3.4 %convert_element_type.15 = bf16[2048,384]{1,0:T(8,128)(2,1)} convert(f32[2048,384]{1,0:T(8,128)} %get-tuple-element.25) | non-fusion elementwise | flops 786432 | bytes 4718592 | tf_op jit(solution)/shard_map/convert_element_type | solution.py:430
  304.3 4.5 %convert_element_type.18 = bf16[2048,512]{1,0:T(8,128)(2,1)} convert(f32[2048,512]{1,0:T(8,128)} %get-tuple-element.27) | non-fusion elementwise | flops 1048576 | bytes 6291456 | tf_op jit(solution)/shard_map/convert_element_type | solution.py:430
  308.8 4.2 %convert_element_type.19 = bf16[512,2048]{1,0:T(8,128)(2,1)} convert(f32[512,2048]{1,0:T(8,128)} %get-tuple-element.28) | non-fusion elementwise | flops 1048576 | bytes 6291456 | tf_op jit(solution)/shard_map/convert_element_type | solution.py:430
  313.0 0.0 copy-done
  313.0 6.2 %copy.15 = bf16[4096,2048]{1,0:T(8,128)(2,1)} copy(bf16[4096,2048]{1,0:T(8,128)(2,1)S(1)} %copy-done) | data formatting | bytes 33554432
  (1 shorter events, 0.0 us)
Async XLA Ops:
  300.9 12.1 %copy-start = (bf16[4096,2048]{1,0:T(8,128)(2,1)S(1)}, bf16[4096,2048]{1,0:T(8,128)(2,1)}, u32[]{:S(2)}) copy-start(bf16[4096,2048]{1,0:T(8,128)(2,1)} %get-tuple-element.36) | copy-start | bytes 50331652

commit v3 on v2

--- a/solution.py
+++ b/solution.py
@@ -14,6 +14,8 @@
 MESH = pl.DeviceIdType.MESH
 CORES = 2
 LOG2E = 1.4426950408889634
+TICKS = 10
+OFFSET = 3
 
 
 def dot_nn(a, b):
@@ -96,17 +98,18 @@
 def layer_kernel(
     nb, nz, q_ref, k_ref, v_ref, kt_ref, vt_ref, dy_ref, n_ref, cos_ref, sin_ref, wo_ref, w1_ref, w2_ref, wqkv_ref, gain_ref, x_hbm, dy_hbm, stat_hbm,
     dx_hbm, gw1_hbm, gwqkv_hbm, gw2_hbm, gwo_hbm,
-    s_ref, dk_acc, dv_acc, ot_acc, dqt_acc, d_out_ref, row_ref, o_ref, dqkv_ref, act_ref, da_ref, acc1, accq, acc2, acco,
-    part, pair, stage, recv, shard, x_rows, dy_rows, stat_rows,
+    s_ref, dk_acc, dv_acc, ot_acc, dqt_acc, d_out_ref, row_ref, o_ref, dqkv_ref, act_ref, da_ref, acc1, accq, acc2, acco, wo_cast,
+    part, pair, stage, recv, shards, x_rows, dy_rows, stat_rows,
     pair_send, pair_recv, rs_send, rs_recv, ag_send, ag_recv, fin_send, fin_recv, load_sem, own_sem, out_sem, credit,
 ):
     hd = q_ref.shape[1]
     scale = hd ** -0.5
-    half = BLK // CORES
-    piece = half // nz
+    sub = BLK // 2
+    quarter = sub // CORES
+    piece = quarter // nz
     hops = nz // 2
     g = pl.program_id(0)
-    i = nb - 1 - g
+    i = jnp.maximum(nb - 1 - g, 0)
 
     me = lax.axis_index("model")
     z, c = lax.div(me, CORES), lax.rem(me, CORES)
@@ -115,9 +118,7 @@
     wrap = lambda n: lax.rem(n + 2 * nz, nz)
     partner = z * CORES + (1 - c)
     toward = tuple(wrap(z + s) * CORES + c for s in signs)
-    compute, reducing, gathering = g < nb, (g >= 1) & (g <= nb), g >= 2
-    red_row = (nb - g) * BLK
-    gat_row = (nb + 1 - g) * BLK
+    compute = g < nb
 
     def at(j):
         return pl.ds(pl.multiple_of(j * BLK, BLK), BLK)
@@ -128,58 +129,56 @@
     def remote(src, dst, send_sem, recv_sem, device):
         return pltpu.make_async_remote_copy(src_ref=src, dst_ref=dst, send_sem=send_sem, recv_sem=recv_sem, device_id={"model": device}, device_id_type=MESH)
 
-    def pair_copy():
-        return remote(part.at[rows((1 - c) * half, half), :], pair, pair_send, pair_recv, partner)
-
-    def rs_copy(flow, s):
-        return remote(stage.at[flow, s - 1], recv.at[flow, s - 1], rs_send.at[flow, s - 1], rs_recv.at[flow, s - 1], toward[flow])
-
-    def mine(p):
-        own = part[rows(c * half + p * piece, piece), :].astype(F32)
-        return own + pair[rows(p * piece, piece), :].astype(F32)
-
-    def rs_start(flow, s, prior):
-        total = mine(wrap(z + signs[flow] * (hops + 1 - s)))
-        if prior:
-            total += recv[flow, s - 2].astype(F32)
-        stage[flow, s - 1] = total.astype(BF)
-        rs_copy(flow, s).start()
-
-    def ag_rows(flow, back):
-        return rows(gat_row + c * half + wrap(z - signs[flow] * back) * piece, piece)
-
-    def ag_copy(flow, s):
-        there = dx_hbm.at[ag_rows(flow, s - 1), :]
-        return remote(shard if s == 1 else there, there, ag_send.at[flow, s - 1], ag_recv.at[flow, s - 1], toward[flow])
-
-    def ag_wait(flow, s):
-        ag_copy(flow, s).wait_send()
-        here = dx_hbm.at[ag_rows(flow, s), :]
-        remote(here, here, ag_send.at[flow, s - 1], ag_recv.at[flow, s - 1], toward[flow]).wait_recv()
-
-    def fin_copy(core):
-        block = dx_hbm.at[rows(gat_row + core * half, half), :]
-        return remote(block, block, fin_send, fin_recv, partner)
-
-    def own_rows(first):
-        return rows(first + c * half + z * piece, piece)
-
-    def loads():
-        at_rows = own_rows(red_row)
-        return [pltpu.make_async_copy(src.at[at_rows, :], dst, load_sem.at[n]) for n, (src, dst) in enumerate(((x_hbm, x_rows), (dy_hbm, dy_rows), (stat_hbm, stat_rows)))]
-
-    def own_store(first):
-        return pltpu.make_async_copy(shard, dx_hbm.at[own_rows(first), :], own_sem)
-
-    def weight_stores():
-        pairs = ((acc1, gw1_hbm), (accq, gwqkv_hbm), (acc2, gw2_hbm), (acco, gwo_hbm))
-        return [pltpu.make_async_copy(src, dst, out_sem.at[n]) for n, (src, dst) in enumerate(pairs)]
-
-    def tick(t):
+    def stream(h, t, ge):
+        reducing, gathering = (ge >= 1) & (ge <= nb), (ge >= 2) & (ge <= nb + 1)
+        red_row = (nb - ge) * BLK + h * sub
+        gat_row = (nb + 1 - ge) * BLK + h * sub
+
+        def pair_copy():
+            return remote(part.at[rows(h * sub + (1 - c) * quarter, quarter), :], pair.at[h], pair_send.at[h], pair_recv.at[h], partner)
+
+        def rs_copy(flow, s):
+            return remote(stage.at[h, flow, s - 1], recv.at[h, flow, s - 1], rs_send.at[h, flow, s - 1], rs_recv.at[h, flow, s - 1], toward[flow])
+
+        def mine(p):
+            own = part[rows(h * sub + c * quarter + p * piece, piece), :].astype(F32)
+            return own + pair[h, rows(p * piece, piece), :].astype(F32)
+
+        def rs_start(flow, s, prior):
+            total = mine(wrap(z + signs[flow] * (hops + 1 - s)))
+            if prior:
+                total += recv[h, flow, s - 2].astype(F32)
+            stage[h, flow, s - 1] = total.astype(BF)
+            rs_copy(flow, s).start()
+
+        def shard(flow, back):
+            return shards.at[h, rows(wrap(z - signs[flow] * back) * piece, piece), :]
+
+        def ag_copy(flow, s):
+            there = shard(flow, s - 1)
+            return remote(there, there, ag_send.at[h, flow, s - 1], ag_recv.at[h, flow, s - 1], toward[flow])
+
+        def ag_wait(flow, s):
+            ag_copy(flow, s).wait_send()
+            here = shard(flow, s)
+            remote(here, here, ag_send.at[h, flow, s - 1], ag_recv.at[h, flow, s - 1], toward[flow]).wait_recv()
+
+        def fin_copy(core):
+            block = dx_hbm.at[rows(gat_row + core * quarter, quarter), :]
+            return remote(shards.at[h], block, fin_send.at[h], fin_recv.at[h], partner)
+
+        def own_store():
+            return pltpu.make_async_copy(shards.at[h], dx_hbm.at[rows(gat_row + c * quarter, quarter), :], own_sem.at[h])
+
+        def loads():
+            at_rows = rows(red_row + c * quarter + z * piece, piece)
+            pairs = ((x_hbm, x_rows), (dy_hbm, dy_rows), (stat_hbm, stat_rows))
+            return [pltpu.make_async_copy(src.at[at_rows, :], dst.at[h], load_sem.at[h, n]) for n, (src, dst) in enumerate(pairs)]
+
         if t == 0:
-            @pl.when(g >= 1)
-            def _():
-                pl.semaphore_wait(credit, 3)
+            @pl.when((ge >= 1) & (ge <= nb + 1))
+            def _():
+                pl.semaphore_wait(credit.at[h], 3)
 
             @pl.when(reducing)
             def _():
@@ -193,6 +192,7 @@
                     ag_copy(flow, 1).start()
         elif t % 2 == 1 and t <= 2 * hops - 1:
             s = (t + 1) // 2
+
             @pl.when(reducing)
             def _():
                 if s == 1:
@@ -206,22 +206,23 @@
                     rs_start(1, s, s > 2)
         elif t % 2 == 0 and t <= 2 * hops:
             s = t // 2
+
             @pl.when(gathering)
             def _():
                 ag_wait(0, s)
                 if s < hops:
                     ag_wait(1, s)
-                if s < hops:
                     ag_copy(0, s + 1).start()
                     if s + 1 < hops:
                         ag_copy(1, s + 1).start()
                 else:
-                    own_store(gat_row).wait()
                     fin_copy(c).start()
+                    own_store().start()
         elif t == 2 * hops + 1:
             @pl.when(gathering)
             def _():
                 fin_copy(c).wait_send()
+                own_store().wait()
                 fin_copy(1 - c).wait_recv()
 
             @pl.when(reducing)
@@ -230,20 +231,44 @@
                     rs_copy(flow, hops).wait()
                 for load in loads():
                     load.wait()
-                total = mine(z) + recv[0, hops - 1].astype(F32) + recv[1, hops - 1].astype(F32)
+                total = mine(z) + recv[h, 0, hops - 1].astype(F32) + recv[h, 1, hops - 1].astype(F32)
                 d = total * gain_ref[...].astype(F32)
-                rstd = stat_rows[:, 1:2]
-                xh = (x_rows[...].astype(F32) - stat_rows[:, 0:1]) * rstd
+                rstd = stat_rows[h, :, 1:2]
+                xh = (x_rows[h].astype(F32) - stat_rows[h, :, 0:1]) * rstd
                 inv = 1.0 / d.shape[1]
                 mean_d = jnp.sum(d, axis=1, keepdims=True) * inv
                 mean_dx = jnp.sum(d * xh, axis=1, keepdims=True) * inv
-                shard[...] = (dy_rows[...].astype(F32) + rstd * (d - mean_d - xh * mean_dx)).astype(BF)
-                own_store(red_row).start()
-
-            @pl.when(g <= nb)
+                shards[h, rows(z * piece, piece), :] = (dy_rows[h].astype(F32) + rstd * (d - mean_d - xh * mean_dx)).astype(BF)
+
+            @pl.when((ge >= 0) & (ge <= nb))
             def _():
                 for device in (partner, *toward):
-                    pl.semaphore_signal(credit, inc=1, device_id={"model": device}, device_id_type=MESH)
+                    pl.semaphore_signal(credit.at[h], inc=1, device_id={"model": device}, device_id_type=MESH)
+
+    def tick(t):
+        stream(0, t, g)
+        if t >= OFFSET:
+            stream(1, t - OFFSET, g)
+        else:
+            stream(1, t - OFFSET + TICKS, g - 1)
+
+    def weight_stores(n):
+        at_rows = rows(n * 512, 512)
+        pairs = ((act_ref, gw1_hbm.at[at_rows, :]), (dqkv_ref, gwqkv_hbm.at[at_rows, :]), (da_ref, gw2_hbm.at[:, at_rows]), (wo_cast, gwo_hbm.at[0, :, at_rows]))
+        return [pltpu.make_async_copy(src, dst, out_sem.at[m]) for m, (src, dst) in enumerate(pairs)]
+
+    def weights_out(n):
+        if n:
+            for store in weight_stores(n - 1):
+                store.wait()
+        if n < acc1.shape[0] // 512:
+            at_rows = rows(n * 512, 512)
+            act_ref[...] = acc1[at_rows, :].astype(BF)
+            dqkv_ref[...] = accq[at_rows, :].astype(BF)
+            da_ref[...] = acc2[:, at_rows].astype(BF)
+            wo_cast[...] = acco[:, at_rows].astype(BF)
+            for store in weight_stores(n):
+                store.start()
 
     def scores():
         d_out_ref[...] = dot_nt(dy_ref[...], wo_ref[0]).astype(BF)
@@ -304,7 +329,7 @@
         dqkv_ref[:, 2 * hd:] = dv_acc[at(i), :].astype(BF)
 
     def mlp(h):
-        r = slice(h * half, (h + 1) * half)
+        r = slice(h * sub, (h + 1) * sub)
         a = dot_nn(n_ref[r, :], w1_ref[...])
         dg = dot_nt(dy_ref[r, :], w2_ref[...])
         cdf = 0.5 * (1.0 + lax.erf(a * 0.7071067811865476))
@@ -332,10 +357,9 @@
 
         lax.fori_loop(0, acc1.shape[0] // 512, step, 0)
 
-    def partial_dn():
-        for h in range(CORES):
-            r = slice(h * half, (h + 1) * half)
-            part[r, :] = (dot_nt(da_ref[r, :], w1_ref[...]) + dot_nt(dqkv_ref[r, :], wqkv_ref[...])).astype(BF)
+    def partial_dn(h):
+        r = slice(h * sub, (h + 1) * sub)
+        part[r, :] = (dot_nt(da_ref[r, :], w1_ref[...]) + dot_nt(dqkv_ref[r, :], wqkv_ref[...])).astype(BF)
 
     @pl.when(g == 0)
     def _():
@@ -345,11 +369,6 @@
         pl.semaphore_wait(barrier, 3)
         for ref in (dk_acc, dv_acc, acc1, accq, acc2, acco):
             ref[...] = jnp.zeros_like(ref)
-
-    @pl.when(g == nb)
-    def _():
-        for store in weight_stores():
-            store.start()
 
     middle = lax.div(i + 1, 2)
     pieces = (
@@ -362,19 +381,24 @@
         lambda: mlp(1),
         lambda: wgrad_down(),
         lambda: wgrad_up(),
-        lambda: partial_dn(),
+        lambda: partial_dn(0),
     )
+    n_out = acc1.shape[0] // 512
     for t, work in enumerate(pieces):
         tick(t)
+        if t == OFFSET - 1:
+            @pl.when((g >= 1) & (g <= nb))
+            def _():
+                partial_dn(1)
 
         @pl.when(compute)
         def _():
             work()
 
-    @pl.when(g == nb + 1)
-    def _():
-        for store in weight_stores():
-            store.wait()
+        if OFFSET <= t <= OFFSET + n_out:
+            @pl.when(g == nb)
+            def _():
+                weights_out(t - OFFSET)
 
 
 def layer_call(mesh, qkv, stat, x, n, dy, wo, w1, w2, wqkv, gain, cos_t, sin_t):
@@ -385,8 +409,9 @@
     nb = t // BLK
     nz = mesh.shape["model"] // CORES
     rot = cos_t.shape[0]
-    half = BLK // CORES
-    piece = half // nz
+    sub = BLK // 2
+    quarter = sub // CORES
+    piece = quarter // nz
     hops = nz // 2
     block = lambda g: jnp.maximum(nb - 1 - g, 0)
     rows = lambda width: pl.BlockSpec((BLK, width), lambda g: (block(g), 0))
@@ -395,19 +420,19 @@
     dma = pltpu.SemaphoreType.DMA
     return pl.pallas_call(
         functools.partial(layer_kernel, nb, nz),
-        grid=(nb + 2,),
+        grid=(nb + 3,),
         in_specs=[rows(hd), whole((t, hd)), whole((t, hd)), whole((hd, t)), whole((hd, t)), rows(d), rows(d), lanes(rot), lanes(rot),
                   whole((1, hd, d)), whole((d, ff)), whole((ff, d)), whole((d, cols)), whole((1, d)), ANY, ANY, ANY],
         out_specs=[ANY] * 5,
-        out_shape=[jax.ShapeDtypeStruct((t, d), BF)] + [jax.ShapeDtypeStruct(s, F32) for s in ((d, ff), (d, cols), (ff, d), (hd, d))],
+        out_shape=[jax.ShapeDtypeStruct(s, BF) for s in ((t, d), (d, ff), (d, cols), (ff, d), (1, hd, d))],
         scratch_shapes=[
             vm((t, BLK), F32), vm((t, hd), F32), vm((t, hd), F32), vm((hd, BLK), F32), vm((hd, BLK), F32),
             vm((BLK, hd), BF), vm((8, BLK), F32), vm((BLK, hd), BF), vm((BLK, cols), BF), vm((BLK, ff), BF), vm((BLK, ff), BF),
-            vm((d, ff), F32), vm((d, cols), F32), vm((ff, d), F32), vm((hd, d), F32),
-            vm((BLK, d), BF), vm((half, d), BF), vm((2, hops, piece, d), BF), vm((2, hops, piece, d), BF), vm((piece, d), BF),
-            vm((piece, d), BF), vm((piece, d), BF), vm((piece, 128), F32),
-            dma, dma, dma((2, hops)), dma((2, hops)), dma((2, hops)), dma((2, hops)), dma, dma, dma((3,)), dma, dma((4,)),
-            pltpu.SemaphoreType.REGULAR,
+            vm((d, ff), F32), vm((d, cols), F32), vm((ff, d), F32), vm((hd, d), F32), vm((hd, 512), BF),
+            vm((BLK, d), BF), vm((2, quarter, d), BF), vm((2, 2, hops, piece, d), BF), vm((2, 2, hops, piece, d), BF), vm((2, quarter, d), BF),
+            vm((2, piece, d), BF), vm((2, piece, d), BF), vm((2, piece, 128), F32),
+            dma((2,)), dma((2,)), dma((2, 2, hops)), dma((2, 2, hops)), dma((2, 2, hops)), dma((2, 2, hops)), dma((2,)), dma((2,)), dma((2, 3)), dma((2,)), dma((4,)),
+            pltpu.SemaphoreType.REGULAR((2,)),
         ],
         compiler_params=pltpu.CompilerParams(dimension_semantics=("arbitrary",), vmem_limit_bytes=VMEM_LIMIT, collective_id=0, has_side_effects=True),
         cost_estimate=cost(2 * t * d * (5 * ff + 3 * cols), 12 * t * d),
@@ -427,7 +452,7 @@
         mean, rstd, gain = ln_mean[None, :], ln_rstd[None, :], ln_gain[None, :]
         normed, *qkv, stat = qkv_call(resid_x, mean, rstd, gain, w_qkv, cos_t, sin_t)
         grad_x, gw_up, gw_qkv, gw_down, gw_out = layer_call(mesh, qkv, stat, resid_x, normed, grad_y, w_out, w_up, w_down, w_qkv, gain, cos_t, sin_t)
-        return grad_x, gw_qkv.astype(BF), gw_out[None].astype(BF), gw_up.astype(BF), gw_down.astype(BF)
+        return grad_x, gw_qkv, gw_out, gw_up, gw_down
 
     in_specs = (P("data", None), P("data"), P("data"), P(None), P("data", None), P(None, "model"), P("model", None, None), P(None, "model"), P("model", None))
     out_specs = (P("data", None), P("data", "model"), P(("data", "model"), None, None), P("data", "model"), P(("data", "model"), None))

time: 320 us -> 306 us (0.956)
  other arithmetic: 16 us -> 1.84 us
  local copies, waits for them, and re-layouts: 7.45 us -> 21.6 us
  Pallas kernels: 295 us -> 281 us
    convert_element_type x4 -> x0, other arithmetic: 14.2 us -> none  [the longest x1 4.54 us: device_step(): gw_up.astype(BF)]
    pallas_call x1, Pallas kernels: 277 us -> 263 us  [layer_call(): pl.pallas_call(functools.partial(layer_kernel, nb, nz), grid=(nb + 3,), i...]
    unnamed x3 -> x13, local copies, waits for them, and re-layouts: 6.16 us -> 20.3 us
where the time goes in v3:
time: 306 us; the launch traced here: 305 us
  Pallas kernels  281 us (92%)
  local copies, waits for them, and re-layouts  21.6 us (7%)
    pallas_call x1, Pallas kernels, layer_call(): pl.pallas_call(functools.partial(layer_kernel, nb, nz), grid=(nb + 3,), i...  263 us
    unnamed x13, local copies, waits for them, and re-layouts  20.3 us
    pallas_call x1, Pallas kernels, qkv_call(): pl.pallas_call(qkv_kernel, grid=(t // BLK,), in_specs=[rows(d), lanes(1),...  17.6 us

profile of v3, /device:TPU:21, one launch (start us, length us, event | category | flops | bytes accessed | tf_op | source)
XLA Modules:
  0.0 305.0 jit_solution(4477777514143082654)
XLA Ops:
  0.6 1.3 broadcast_in_dim.13.g_ref.gain_ref
  1.9 1.8 fusion
  3.8 17.6 %ln_qkv.1 = (bf16[4096,2048]{1,0:T(8,128)(2,1)}, bf16[4096,128]{1,0:T(8,128)(2,1)}, bf16[4096,128]{1,0:T(8,128)(2,1)}, bf16[4096,128]{1,0:T(8,128)(2,1)}, bf16[1...) custom-call(bf16[4096,2048]{1,0:T(8,128)(2,1)} %x_hbm.1, f32[1,4096]{1,0:T(1,128)} %bitcast.2, ...), custom_call_target="tpu_custom_call" | custom-call | flops 6442450944 | bytes 33554432 | tf_op jit(solution)/shard_map/ln_qkv/pallas_call | solution.py:86
  21.4 263.3 %layer_backward.1 = (bf16[4096,2048]{1,0:T(8,128)(2,1)}, bf16[2048,512]{1,0:T(8,128)(2,1)}, bf16[2048,384]{1,0:T(8,128)(2,1)}, bf16[512,2048]{1,0:T(8,128)(2,1)}, bf16[1,128,2048]{2,1,0:T(8,128)(2,1)}) custom-call(bf16[4096,128]{1,0:T(8,128)(2,1)} %get-tuple-element.17.q_ref, bf16[4096,128]{1,0:T(8,128)(2,1)} %get-tuple-element.18.k_ref, ...), custom_call_target="tpu_custom_call" | custom-call | flops 62277025792 | bytes 100663296 | tf_op jit(solution)/shard_map/layer_backward/pallas_call | solution.py:421
  284.7 0.0 copy-start.2
  284.7 14.3 %copy.19 = bf16[4096,2048]{1,0:T(8,128)(2,1)} copy(bf16[4096,2048]{1,0:T(8,128)(2,1)} %get-tuple-element.36) | data formatting | bytes 33554432
  299.0 0.0 copy-done.2
  299.0 0.0 copy-start.3
  299.0 0.0 copy-start.1
  299.0 1.1 copy.20
  300.1 0.2 copy-done.3
  300.3 0.8 copy.21
  301.1 0.2 copy-done.1
  301.3 0.0 copy-start
  301.3 1.3 copy.22
  302.6 1.0 copy-done
  303.7 1.3 copy.23
  (1 shorter events, 0.0 us)
Async XLA Ops:
  284.7 14.3 %copy-start.2 = (bf16[2048,384]{1,0:T(8,128)(2,1)S(1)}, bf16[2048,384]{1,0:T(8,128)(2,1)}, u32[]{:S(2)}) copy-start(bf16[2048,384]{1,0:T(8,128)(2,1)} %get-tuple-element.37) | copy-start | bytes 4718596
  299.0 1.4 copy-start.3
  299.0 2.3 copy-start.1
  301.3 2.3 copy-start

commit v4 on v3

--- a/solution.py
+++ b/solution.py
@@ -58,21 +58,23 @@
 
 def qkv_kernel(x_ref, mean_ref, rstd_ref, g_ref, w_ref, cos_ref, sin_ref, n_ref, q_ref, k_ref, v_ref, kt_ref, vt_ref, stat_ref):
     hd = q_ref.shape[1]
-    mean, rstd = column(mean_ref[...]), column(rstd_ref[...])
-    lane = lax.broadcasted_iota(jnp.int32, stat_ref.shape, 1)
-    stat_ref[...] = jnp.where(lane == 0, mean, rstd)
-    xh = (x_ref[...].astype(F32) - mean) * rstd
-    n = (xh * g_ref[...].astype(F32)).astype(BF)
-    n_ref[...] = n
-    proj = dot_nn(n, w_ref[...])
-    cos_t, sin_t = cos_ref[...], sin_ref[...]
-    q_ref[...] = rotate_t(proj[:, :hd].T, cos_t, sin_t).T.astype(BF)
-    kt = rotate_t(proj[:, hd:2 * hd].T, cos_t, sin_t)
-    kt_ref[...] = kt.astype(BF)
-    k_ref[...] = kt.T.astype(BF)
-    v = proj[:, 2 * hd:]
-    v_ref[...] = v.astype(BF)
-    vt_ref[...] = v.T.astype(BF)
+    gain = g_ref[...].astype(F32)
+    for part in range(2):
+        r = slice(part * BLK // 2, (part + 1) * BLK // 2)
+        mean, rstd = column(mean_ref[:, r]), column(rstd_ref[:, r])
+        lane = lax.broadcasted_iota(jnp.int32, (BLK // 2, stat_ref.shape[1]), 1)
+        stat_ref[r, :] = jnp.where(lane == 0, mean, rstd)
+        n = ((x_ref[r, :].astype(F32) - mean) * rstd * gain).astype(BF)
+        n_ref[r, :] = n
+        proj = dot_nn(n, w_ref[...])
+        cos_t, sin_t = cos_ref[:, r], sin_ref[:, r]
+        q_ref[r, :] = rotate_t(proj[:, :hd].T, cos_t, sin_t).T.astype(BF)
+        kt = rotate_t(proj[:, hd:2 * hd].T, cos_t, sin_t)
+        kt_ref[:, r] = kt.astype(BF)
+        k_ref[r, :] = kt.T.astype(BF)
+        v = proj[:, 2 * hd:]
+        v_ref[r, :] = v.astype(BF)
+        vt_ref[:, r] = v.T.astype(BF)
 
 
 def qkv_call(x, mean, rstd, g, w, cos_t, sin_t):
@@ -129,56 +131,61 @@
     def remote(src, dst, send_sem, recv_sem, device):
         return pltpu.make_async_remote_copy(src_ref=src, dst_ref=dst, send_sem=send_sem, recv_sem=recv_sem, device_id={"model": device}, device_id_type=MESH)
 
-    def stream(h, t, ge):
-        reducing, gathering = (ge >= 1) & (ge <= nb), (ge >= 2) & (ge <= nb + 1)
-        red_row = (nb - ge) * BLK + h * sub
-        gat_row = (nb + 1 - ge) * BLK + h * sub
+    def part_slot(h, b):
+        return lax.rem(b + 6, 2) if h == 0 else 2 + lax.rem(b + 6, 3)
+
+    def stream(h, t, b):
+        reducing, gathering = (b >= 0) & (b < nb), (b >= 2) & (b < nb + 2)
+        red_row = (nb - 1 - b) * BLK + h * sub
+        gat_row = (nb + 1 - b) * BLK + h * sub
+        held = part_slot(h, b)
+        k = 2 * h + lax.rem(b + 6, 2)
 
         def pair_copy():
-            return remote(part.at[rows(h * sub + (1 - c) * quarter, quarter), :], pair.at[h], pair_send.at[h], pair_recv.at[h], partner)
+            return remote(part.at[held, rows((1 - c) * quarter, quarter), :], pair.at[k], pair_send.at[k], pair_recv.at[k], partner)
 
         def rs_copy(flow, s):
-            return remote(stage.at[h, flow, s - 1], recv.at[h, flow, s - 1], rs_send.at[h, flow, s - 1], rs_recv.at[h, flow, s - 1], toward[flow])
+            return remote(stage.at[k, flow, (s - 1) % 2], recv.at[k, flow, s - 1], rs_send.at[k, flow, s - 1], rs_recv.at[k, flow, s - 1], toward[flow])
 
         def mine(p):
-            own = part[rows(h * sub + c * quarter + p * piece, piece), :].astype(F32)
-            return own + pair[h, rows(p * piece, piece), :].astype(F32)
+            own = part[held, rows(c * quarter + p * piece, piece), :].astype(F32)
+            return own + pair[k, rows(p * piece, piece), :].astype(F32)
 
         def rs_start(flow, s, prior):
             total = mine(wrap(z + signs[flow] * (hops + 1 - s)))
             if prior:
-                total += recv[h, flow, s - 2].astype(F32)
-            stage[h, flow, s - 1] = total.astype(BF)
+                total += recv[k, flow, s - 2].astype(F32)
+            stage[k, flow, (s - 1) % 2] = total.astype(BF)
             rs_copy(flow, s).start()
 
         def shard(flow, back):
-            return shards.at[h, rows(wrap(z - signs[flow] * back) * piece, piece), :]
+            return shards.at[k, rows(wrap(z - signs[flow] * back) * piece, piece), :]
 
         def ag_copy(flow, s):
             there = shard(flow, s - 1)
-            return remote(there, there, ag_send.at[h, flow, s - 1], ag_recv.at[h, flow, s - 1], toward[flow])
+            return remote(there, there, ag_send.at[k, flow, s - 1], ag_recv.at[k, flow, s - 1], toward[flow])
 
         def ag_wait(flow, s):
             ag_copy(flow, s).wait_send()
             here = shard(flow, s)
-            remote(here, here, ag_send.at[h, flow, s - 1], ag_recv.at[h, flow, s - 1], toward[flow]).wait_recv()
+            remote(here, here, ag_send.at[k, flow, s - 1], ag_recv.at[k, flow, s - 1], toward[flow]).wait_recv()
 
         def fin_copy(core):
             block = dx_hbm.at[rows(gat_row + core * quarter, quarter), :]
-            return remote(shards.at[h], block, fin_send.at[h], fin_recv.at[h], partner)
+            return remote(shards.at[k], block, fin_send.at[k], fin_recv.at[k], partner)
 
         def own_store():
-            return pltpu.make_async_copy(shards.at[h], dx_hbm.at[rows(gat_row + c * quarter, quarter), :], own_sem.at[h])
+            return pltpu.make_async_copy(shards.at[k], dx_hbm.at[rows(gat_row + c * quarter, quarter), :], own_sem.at[k])
 
         def loads():
             at_rows = rows(red_row + c * quarter + z * piece, piece)
             pairs = ((x_hbm, x_rows), (dy_hbm, dy_rows), (stat_hbm, stat_rows))
-            return [pltpu.make_async_copy(src.at[at_rows, :], dst.at[h], load_sem.at[h, n]) for n, (src, dst) in enumerate(pairs)]
+            return [pltpu.make_async_copy(src.at[at_rows, :], dst.at[k], load_sem.at[k, n]) for n, (src, dst) in enumerate(pairs)]
 
         if t == 0:
-            @pl.when((ge >= 1) & (ge <= nb + 1))
-            def _():
-                pl.semaphore_wait(credit.at[h], 3)
+            @pl.when(gathering)
+            def _():
+                pl.semaphore_wait(credit.at[k], 3)
 
             @pl.when(reducing)
             def _():
@@ -231,26 +238,28 @@
                     rs_copy(flow, hops).wait()
                 for load in loads():
                     load.wait()
-                total = mine(z) + recv[h, 0, hops - 1].astype(F32) + recv[h, 1, hops - 1].astype(F32)
+                total = mine(z) + recv[k, 0, hops - 1].astype(F32) + recv[k, 1, hops - 1].astype(F32)
                 d = total * gain_ref[...].astype(F32)
-                rstd = stat_rows[h, :, 1:2]
-                xh = (x_rows[h].astype(F32) - stat_rows[h, :, 0:1]) * rstd
+                rstd = stat_rows[k, :, 1:2]
+                xh = (x_rows[k].astype(F32) - stat_rows[k, :, 0:1]) * rstd
                 inv = 1.0 / d.shape[1]
                 mean_d = jnp.sum(d, axis=1, keepdims=True) * inv
                 mean_dx = jnp.sum(d * xh, axis=1, keepdims=True) * inv
-                shards[h, rows(z * piece, piece), :] = (dy_rows[h].astype(F32) + rstd * (d - mean_d - xh * mean_dx)).astype(BF)
-
-            @pl.when((ge >= 0) & (ge <= nb))
+                shards[k, rows(z * piece, piece), :] = (dy_rows[k].astype(F32) + rstd * (d - mean_d - xh * mean_dx)).astype(BF)
+
+            @pl.when(reducing)
             def _():
                 for device in (partner, *toward):
-                    pl.semaphore_signal(credit.at[h], inc=1, device_id={"model": device}, device_id_type=MESH)
+                    pl.semaphore_signal(credit.at[k], inc=1, device_id={"model": device}, device_id_type=MESH)
 
     def tick(t):
-        stream(0, t, g)
-        if t >= OFFSET:
-            stream(1, t - OFFSET, g)
-        else:
-            stream(1, t - OFFSET + TICKS, g - 1)
+        for h in range(2):
+            late = t - OFFSET * h
+            step = g if late >= 0 else g - 1
+            late %= TICKS
+            if late % 2 == 0:
+                stream(h, late // 2, step - 1)
+                stream(h, (TICKS + late) // 2, step - 2)
 
     def weight_stores(n):
         at_rows = rows(n * 512, 512)
@@ -329,13 +338,14 @@
         dqkv_ref[:, 2 * hd:] = dv_acc[at(i), :].astype(BF)
 
     def mlp(h):
-        r = slice(h * sub, (h + 1) * sub)
-        a = dot_nn(n_ref[r, :], w1_ref[...])
-        dg = dot_nt(dy_ref[r, :], w2_ref[...])
+        width = w1_ref.shape[1] // 2
+        at_cols = slice(h * width, (h + 1) * width)
+        a = dot_nn(n_ref[...], w1_ref[:, at_cols])
+        dg = dot_nt(dy_ref[...], w2_ref[at_cols, :])
         cdf = 0.5 * (1.0 + lax.erf(a * 0.7071067811865476))
-        act_ref[r, :] = (a * cdf).astype(BF)
+        act_ref[:, at_cols] = (a * cdf).astype(BF)
         pdf = jnp.exp(a * a * -0.5) * 0.3989422804014327
-        da_ref[r, :] = (dg * (cdf + a * pdf)).astype(BF)
+        da_ref[:, at_cols] = (dg * (cdf + a * pdf)).astype(BF)
 
     def wgrad_down():
         def step(n, carry):
@@ -357,9 +367,17 @@
 
         lax.fori_loop(0, acc1.shape[0] // 512, step, 0)
 
-    def partial_dn(h):
-        r = slice(h * sub, (h + 1) * sub)
-        part[r, :] = (dot_nt(da_ref[r, :], w1_ref[...]) + dot_nt(dqkv_ref[r, :], wqkv_ref[...])).astype(BF)
+    def partial_dn():
+        first, second = part_slot(0, g), part_slot(1, g)
+
+        def step(n, carry):
+            cols = rows(n * 512, 512)
+            dn = (dot_nt(da_ref[...], w1_ref[cols, :]) + dot_nt(dqkv_ref[...], wqkv_ref[cols, :])).astype(BF)
+            part[first, :, cols] = dn[:sub]
+            part[second, :, cols] = dn[sub:]
+            return carry
+
+        lax.fori_loop(0, part.shape[2] // 512, step, 0)
 
     @pl.when(g == 0)
     def _():
@@ -381,24 +399,20 @@
         lambda: mlp(1),
         lambda: wgrad_down(),
         lambda: wgrad_up(),
-        lambda: partial_dn(0),
+        lambda: partial_dn(),
     )
     n_out = acc1.shape[0] // 512
     for t, work in enumerate(pieces):
         tick(t)
-        if t == OFFSET - 1:
-            @pl.when((g >= 1) & (g <= nb))
-            def _():
-                partial_dn(1)
 
         @pl.when(compute)
         def _():
             work()
 
-        if OFFSET <= t <= OFFSET + n_out:
+        if t <= n_out:
             @pl.when(g == nb)
             def _():
-                weights_out(t - OFFSET)
+                weights_out(t)
 
 
 def layer_call(mesh, qkv, stat, x, n, dy, wo, w1, w2, wqkv, gain, cos_t, sin_t):
@@ -420,7 +434,7 @@
     dma = pltpu.SemaphoreType.DMA
     return pl.pallas_call(
         functools.partial(layer_kernel, nb, nz),
-        grid=(nb + 3,),
+        grid=(nb + 5,),
         in_specs=[rows(hd), whole((t, hd)), whole((t, hd)), whole((hd, t)), whole((hd, t)), rows(d), rows(d), lanes(rot), lanes(rot),
                   whole((1, hd, d)), whole((d, ff)), whole((ff, d)), whole((d, cols)), whole((1, d)), ANY, ANY, ANY],
         out_specs=[ANY] * 5,
@@ -429,10 +443,10 @@
             vm((t, BLK), F32), vm((t, hd), F32), vm((t, hd), F32), vm((hd, BLK), F32), vm((hd, BLK), F32),
             vm((BLK, hd), BF), vm((8, BLK), F32), vm((BLK, hd), BF), vm((BLK, cols), BF), vm((BLK, ff), BF), vm((BLK, ff), BF),
             vm((d, ff), F32), vm((d, cols), F32), vm((ff, d), F32), vm((hd, d), F32), vm((hd, 512), BF),
-            vm((BLK, d), BF), vm((2, quarter, d), BF), vm((2, 2, hops, piece, d), BF), vm((2, 2, hops, piece, d), BF), vm((2, quarter, d), BF),
-            vm((2, piece, d), BF), vm((2, piece, d), BF), vm((2, piece, 128), F32),
-            dma((2,)), dma((2,)), dma((2, 2, hops)), dma((2, 2, hops)), dma((2, 2, hops)), dma((2, 2, hops)), dma((2,)), dma((2,)), dma((2, 3)), dma((2,)), dma((4,)),
-            pltpu.SemaphoreType.REGULAR((2,)),
+            vm((5, sub, d), BF), vm((4, quarter, d), BF), vm((4, 2, 2, piece, d), BF), vm((4, 2, hops, piece, d), BF), vm((4, quarter, d), BF),
+            vm((4, piece, d), BF), vm((4, piece, d), BF), vm((4, piece, 128), F32),
+            dma((4,)), dma((4,)), dma((4, 2, hops)), dma((4, 2, hops)), dma((4, 2, hops)), dma((4, 2, hops)), dma((4,)), dma((4,)), dma((4, 3)), dma((4,)), dma((4,)),
+            pltpu.SemaphoreType.REGULAR((4,)),
         ],
         compiler_params=pltpu.CompilerParams(dimension_semantics=("arbitrary",), vmem_limit_bytes=VMEM_LIMIT, collective_id=0, has_side_effects=True),
         cost_estimate=cost(2 * t * d * (5 * ff + 3 * cols), 12 * t * d),

time: 306 us -> 290 us (0.948)
  Pallas kernels: 281 us -> 265 us
    pallas_call x1, Pallas kernels: 263 us -> 245 us  [layer_call(): pl.pallas_call(functools.partial(layer_kernel, nb, nz), grid=(nb + 5,), i...]
where the time goes in v4:
time: 290 us; the launch traced here: 289 us
  Pallas kernels  265 us (91%)
  local copies, waits for them, and re-layouts  21.6 us (7%)
    pallas_call x1, Pallas kernels, layer_call(): pl.pallas_call(functools.partial(layer_kernel, nb, nz), grid=(nb + 5,), i...  245 us
    unnamed x13, local copies, waits for them, and re-layouts  20.3 us
    pallas_call x1, Pallas kernels, qkv_call(): pl.pallas_call(qkv_kernel, grid=(t // BLK,), in_specs=[rows(d), lanes(1),...  20.2 us

profile of v4, /device:TPU:21, one launch (start us, length us, event | category | flops | bytes accessed | tf_op | source)
XLA Modules:
  0.0 289.0 jit_solution(7320751484010044096)
XLA Ops:
  0.6 1.3 broadcast_in_dim.13.g_ref.gain_ref
  1.9 1.8 fusion
  3.8 20.2 %ln_qkv.1 = (bf16[4096,2048]{1,0:T(8,128)(2,1)}, bf16[4096,128]{1,0:T(8,128)(2,1)}, bf16[4096,128]{1,0:T(8,128)(2,1)}, bf16[4096,128]{1,0:T(8,128)(2,1)}, bf16[1...) custom-call(bf16[4096,2048]{1,0:T(8,128)(2,1)} %x_hbm.1, f32[1,4096]{1,0:T(1,128)} %bitcast.2, ...), custom_call_target="tpu_custom_call" | custom-call | flops 6442450944 | bytes 33554432 | tf_op jit(solution)/shard_map/ln_qkv/pallas_call | solution.py:88
  24.0 244.8 %layer_backward.1 = (bf16[4096,2048]{1,0:T(8,128)(2,1)}, bf16[2048,512]{1,0:T(8,128)(2,1)}, bf16[2048,384]{1,0:T(8,128)(2,1)}, bf16[512,2048]{1,0:T(8,128)(2,1)}, bf16[1,128,2048]{2,1,0:T(8,128)(2,1)}) custom-call(bf16[4096,128]{1,0:T(8,128)(2,1)} %get-tuple-element.17.q_ref, bf16[4096,128]{1,0:T(8,128)(2,1)} %get-tuple-element.18.k_ref, ...), custom_call_target="tpu_custom_call" | custom-call | flops 62277025792 | bytes 100663296 | tf_op jit(solution)/shard_map/layer_backward/pallas_call | solution.py:435
  268.7 0.0 copy-start.2
  268.8 14.3 %copy.19 = bf16[4096,2048]{1,0:T(8,128)(2,1)} copy(bf16[4096,2048]{1,0:T(8,128)(2,1)} %get-tuple-element.36) | data formatting | bytes 33554432
  283.0 0.0 copy-done.2
  283.0 0.0 copy-start.3
  283.0 0.0 copy-start.1
  283.0 1.1 copy.20
  284.2 0.2 copy-done.3
  284.4 0.8 copy.21
  285.2 0.2 copy-done.1
  285.4 0.0 copy-start
  285.4 1.3 copy.22
  286.7 1.0 copy-done
  287.7 1.3 copy.23
  (1 shorter events, 0.0 us)
Async XLA Ops:
  268.7 14.3 %copy-start.2 = (bf16[2048,384]{1,0:T(8,128)(2,1)S(1)}, bf16[2048,384]{1,0:T(8,128)(2,1)}, u32[]{:S(2)}) copy-start(bf16[2048,384]{1,0:T(8,128)(2,1)} %get-tuple-element.37) | copy-start | bytes 4718596
  283.0 1.4 copy-start.3
  283.0 2.3 copy-start.1
  285.4 2.3 copy-start

commit v5 on v4

--- a/solution.py
+++ b/solution.py
@@ -15,6 +15,7 @@
 CORES = 2
 LOG2E = 1.4426950408889634
 TICKS = 10
+PUT_OFF = 2
 OFFSET = 3
 
 
@@ -58,23 +59,21 @@
 
 def qkv_kernel(x_ref, mean_ref, rstd_ref, g_ref, w_ref, cos_ref, sin_ref, n_ref, q_ref, k_ref, v_ref, kt_ref, vt_ref, stat_ref):
     hd = q_ref.shape[1]
-    gain = g_ref[...].astype(F32)
-    for part in range(2):
-        r = slice(part * BLK // 2, (part + 1) * BLK // 2)
-        mean, rstd = column(mean_ref[:, r]), column(rstd_ref[:, r])
-        lane = lax.broadcasted_iota(jnp.int32, (BLK // 2, stat_ref.shape[1]), 1)
-        stat_ref[r, :] = jnp.where(lane == 0, mean, rstd)
-        n = ((x_ref[r, :].astype(F32) - mean) * rstd * gain).astype(BF)
-        n_ref[r, :] = n
-        proj = dot_nn(n, w_ref[...])
-        cos_t, sin_t = cos_ref[:, r], sin_ref[:, r]
-        q_ref[r, :] = rotate_t(proj[:, :hd].T, cos_t, sin_t).T.astype(BF)
-        kt = rotate_t(proj[:, hd:2 * hd].T, cos_t, sin_t)
-        kt_ref[:, r] = kt.astype(BF)
-        k_ref[r, :] = kt.T.astype(BF)
-        v = proj[:, 2 * hd:]
-        v_ref[r, :] = v.astype(BF)
-        vt_ref[:, r] = v.T.astype(BF)
+    mean, rstd = column(mean_ref[...]), column(rstd_ref[...])
+    lane = lax.broadcasted_iota(jnp.int32, stat_ref.shape, 1)
+    stat_ref[...] = jnp.where(lane == 0, mean, rstd)
+    xh = (x_ref[...].astype(F32) - mean) * rstd
+    n = (xh * g_ref[...].astype(F32)).astype(BF)
+    n_ref[...] = n
+    proj = dot_nn(n, w_ref[...])
+    cos_t, sin_t = cos_ref[...], sin_ref[...]
+    q_ref[...] = rotate_t(proj[:, :hd].T, cos_t, sin_t).T.astype(BF)
+    kt = rotate_t(proj[:, hd:2 * hd].T, cos_t, sin_t)
+    kt_ref[...] = kt.astype(BF)
+    k_ref[...] = kt.T.astype(BF)
+    v = proj[:, 2 * hd:]
+    v_ref[...] = v.astype(BF)
+    vt_ref[...] = v.T.astype(BF)
 
 
 def qkv_call(x, mean, rstd, g, w, cos_t, sin_t):
@@ -121,6 +120,7 @@
     partner = z * CORES + (1 - c)
     toward = tuple(wrap(z + s) * CORES + c for s in signs)
     compute = g < nb
+    slot = jnp.minimum(g, PUT_OFF)
 
     def at(j):
         return pl.ds(pl.multiple_of(j * BLK, BLK), BLK)
@@ -263,7 +263,7 @@
 
     def weight_stores(n):
         at_rows = rows(n * 512, 512)
-        pairs = ((act_ref, gw1_hbm.at[at_rows, :]), (dqkv_ref, gwqkv_hbm.at[at_rows, :]), (da_ref, gw2_hbm.at[:, at_rows]), (wo_cast, gwo_hbm.at[0, :, at_rows]))
+        pairs = ((act_ref.at[PUT_OFF], gw1_hbm.at[at_rows, :]), (dqkv_ref.at[PUT_OFF], gwqkv_hbm.at[at_rows, :]), (da_ref.at[PUT_OFF], gw2_hbm.at[:, at_rows]), (wo_cast, gwo_hbm.at[0, :, at_rows]))
         return [pltpu.make_async_copy(src, dst, out_sem.at[m]) for m, (src, dst) in enumerate(pairs)]
 
     def weights_out(n):
@@ -272,9 +272,9 @@
                 store.wait()
         if n < acc1.shape[0] // 512:
             at_rows = rows(n * 512, 512)
-            act_ref[...] = acc1[at_rows, :].astype(BF)
-            dqkv_ref[...] = accq[at_rows, :].astype(BF)
-            da_ref[...] = acc2[:, at_rows].astype(BF)
+            act_ref[PUT_OFF] = acc1[at_rows, :].astype(BF)
+            dqkv_ref[PUT_OFF] = accq[at_rows, :].astype(BF)
+            da_ref[PUT_OFF] = acc2[:, at_rows].astype(BF)
             wo_cast[...] = acco[:, at_rows].astype(BF)
             for store in weight_stores(n):
                 store.start()
@@ -316,7 +316,7 @@
 
     def delta():
         row_ref[1:2, :] = jnp.sum(ot_acc[...] * d_out_ref[...].astype(F32).T, axis=0, keepdims=True)
-        o_ref[...] = ot_acc[...].T.astype(BF)
+        o_ref[slot] = ot_acc[...].T.astype(BF)
 
     def grads(first, last):
         m, delta = row_ref[0:1, :], row_ref[1:2, :]
@@ -333,9 +333,9 @@
 
     def heads_done():
         cos_t, sin_t = cos_ref[...], sin_ref[...]
-        dqkv_ref[:, :hd] = rotate_t(dqt_acc[...], cos_t, -sin_t).T.astype(BF)
-        dqkv_ref[:, hd:2 * hd] = rotate_t(dk_acc[at(i), :].T, cos_t, -sin_t).T.astype(BF)
-        dqkv_ref[:, 2 * hd:] = dv_acc[at(i), :].astype(BF)
+        dqkv_ref[slot, :, :hd] = rotate_t(dqt_acc[...], cos_t, -sin_t).T.astype(BF)
+        dqkv_ref[slot, :, hd:2 * hd] = rotate_t(dk_acc[at(i), :].T, cos_t, -sin_t).T.astype(BF)
+        dqkv_ref[slot, :, 2 * hd:] = dv_acc[at(i), :].astype(BF)
 
     def mlp(h):
         width = w1_ref.shape[1] // 2
@@ -343,36 +343,33 @@
         a = dot_nn(n_ref[...], w1_ref[:, at_cols])
         dg = dot_nt(dy_ref[...], w2_ref[at_cols, :])
         cdf = 0.5 * (1.0 + lax.erf(a * 0.7071067811865476))
-        act_ref[:, at_cols] = (a * cdf).astype(BF)
+        act_ref[slot, :, at_cols] = (a * cdf).astype(BF)
         pdf = jnp.exp(a * a * -0.5) * 0.3989422804014327
-        da_ref[:, at_cols] = (dg * (cdf + a * pdf)).astype(BF)
-
-    def wgrad_down():
+        da_ref[slot, :, at_cols] = (dg * (cdf + a * pdf)).astype(BF)
+
+    def down_step(n, used):
+        cols = rows(n * 512, 512)
+        dy = dy_ref[:, cols]
+        acc2[:, cols] += dot_tn(act_ref[used], dy)
+        acco[:, cols] += dot_tn(o_ref[used], dy)
+
+    def up_step(n, used):
+        down = rows(n * 512, 512)
+        x = n_ref[:, down]
+        acc1[down, :] += dot_tn(x, da_ref[used])
+        accq[down, :] += dot_tn(x, dqkv_ref[used])
+
+    n_out = acc1.shape[0] // 512
+
+    def each(step):
+        lax.fori_loop(0, n_out, lambda n, carry: (step(n, PUT_OFF), carry)[1], 0)
+
+    def partial_dn():
+        first, second = part_slot(0, g), part_slot(1, g)
+
         def step(n, carry):
             cols = rows(n * 512, 512)
-            dy = dy_ref[:, cols]
-            acc2[:, cols] += dot_tn(act_ref[...], dy)
-            acco[:, cols] += dot_tn(o_ref[...], dy)
-            return carry
-
-        lax.fori_loop(0, acc2.shape[1] // 512, step, 0)
-
-    def wgrad_up():
-        def step(n, carry):
-            down = rows(n * 512, 512)
-            x = n_ref[:, down]
-            acc1[down, :] += dot_tn(x, da_ref[...])
-            accq[down, :] += dot_tn(x, dqkv_ref[...])
-            return carry
-
-        lax.fori_loop(0, acc1.shape[0] // 512, step, 0)
-
-    def partial_dn():
-        first, second = part_slot(0, g), part_slot(1, g)
-
-        def step(n, carry):
-            cols = rows(n * 512, 512)
-            dn = (dot_nt(da_ref[...], w1_ref[cols, :]) + dot_nt(dqkv_ref[...], wqkv_ref[cols, :])).astype(BF)
+            dn = (dot_nt(da_ref[slot], w1_ref[cols, :]) + dot_nt(dqkv_ref[slot], wqkv_ref[cols, :])).astype(BF)
             part[first, :, cols] = dn[:sub]
             part[second, :, cols] = dn[sub:]
             return carry
@@ -389,28 +386,33 @@
             ref[...] = jnp.zeros_like(ref)
 
     middle = lax.div(i + 1, 2)
+    late = compute & (g >= PUT_OFF)
     pieces = (
-        lambda: scores(),
-        lambda: probs(0, middle),
-        lambda: (probs(middle, i + 1), delta()),
-        lambda: grads(0, middle),
-        lambda: (grads(middle, i + 1), heads_done()),
-        lambda: mlp(0),
-        lambda: mlp(1),
-        lambda: wgrad_down(),
-        lambda: wgrad_up(),
-        lambda: partial_dn(),
+        (compute, lambda: scores()),
+        (compute, lambda: probs(0, middle)),
+        (compute, lambda: (probs(middle, i + 1), delta())),
+        (compute, lambda: grads(0, middle)),
+        (compute, lambda: (grads(middle, i + 1), heads_done())),
+        (compute, lambda: mlp(0)),
+        (compute, lambda: mlp(1)),
+        (late, lambda: each(down_step)),
+        (late, lambda: each(up_step)),
+        (compute, lambda: partial_dn()),
     )
-    n_out = acc1.shape[0] // 512
-    for t, work in enumerate(pieces):
+    for t, (when, work) in enumerate(pieces):
         tick(t)
 
-        @pl.when(compute)
+        @pl.when(when)
         def _():
             work()
 
+        if t < 2 * n_out:
+            @pl.when((g >= nb) & (g < nb + PUT_OFF))
+            def _():
+                (down_step if t < n_out else up_step)(t % n_out, g - nb)
+
         if t <= n_out:
-            @pl.when(g == nb)
+            @pl.when(g == nb + PUT_OFF)
             def _():
                 weights_out(t)
 
@@ -428,20 +430,22 @@
     piece = quarter // nz
     hops = nz // 2
     block = lambda g: jnp.maximum(nb - 1 - g, 0)
+    again = lambda g: jnp.where(g < nb, nb - 1 - g, nb - 1 - jnp.minimum(g - nb, PUT_OFF - 1))
     rows = lambda width: pl.BlockSpec((BLK, width), lambda g: (block(g), 0))
+    twice = lambda width: pl.BlockSpec((BLK, width), lambda g: (again(g), 0))
     lanes = lambda height: pl.BlockSpec((height, BLK), lambda g: (0, block(g)))
     vm = pltpu.VMEM
     dma = pltpu.SemaphoreType.DMA
     return pl.pallas_call(
         functools.partial(layer_kernel, nb, nz),
         grid=(nb + 5,),
-        in_specs=[rows(hd), whole((t, hd)), whole((t, hd)), whole((hd, t)), whole((hd, t)), rows(d), rows(d), lanes(rot), lanes(rot),
+        in_specs=[rows(hd), whole((t, hd)), whole((t, hd)), whole((hd, t)), whole((hd, t)), twice(d), twice(d), lanes(rot), lanes(rot),
                   whole((1, hd, d)), whole((d, ff)), whole((ff, d)), whole((d, cols)), whole((1, d)), ANY, ANY, ANY],
         out_specs=[ANY] * 5,
         out_shape=[jax.ShapeDtypeStruct(s, BF) for s in ((t, d), (d, ff), (d, cols), (ff, d), (1, hd, d))],
         scratch_shapes=[
             vm((t, BLK), F32), vm((t, hd), F32), vm((t, hd), F32), vm((hd, BLK), F32), vm((hd, BLK), F32),
-            vm((BLK, hd), BF), vm((8, BLK), F32), vm((BLK, hd), BF), vm((BLK, cols), BF), vm((BLK, ff), BF), vm((BLK, ff), BF),
+            vm((BLK, hd), BF), vm((8, BLK), F32), vm((PUT_OFF + 1, BLK, hd), BF), vm((PUT_OFF + 1, BLK, cols), BF), vm((PUT_OFF + 1, BLK, ff), BF), vm((PUT_OFF + 1, BLK, ff), BF),
             vm((d, ff), F32), vm((d, cols), F32), vm((ff, d), F32), vm((hd, d), F32), vm((hd, 512), BF),
             vm((5, sub, d), BF), vm((4, quarter, d), BF), vm((4, 2, 2, piece, d), BF), vm((4, 2, hops, piece, d), BF), vm((4, quarter, d), BF),
             vm((4, piece, d), BF), vm((4, piece, d), BF), vm((4, piece, 128), F32),
@@ -452,6 +456,31 @@
         cost_estimate=cost(2 * t * d * (5 * ff + 3 * cols), 12 * t * d),
         name="layer_backward",
     )(q, k, v, kt, vt, dy, n, cos_t, sin_t, wo, w1, w2, wqkv, gain, x, dy, stat)
+
+
+def copy_kernel(*refs):
+    n = len(refs) // 2
+    for src, dst in zip(refs[:n], refs[n:]):
+        dst[...] = src[...]
+
+
+def copy_call(arrays):
+    steps = 8
+
+    def spec(a):
+        shape = (*a.shape[:-2], a.shape[-2] // steps, a.shape[-1])
+        return pl.BlockSpec(shape, lambda i: (*(0,) * (len(shape) - 2), i, 0))
+
+    specs = [spec(a) for a in arrays]
+    return pl.pallas_call(
+        copy_kernel,
+        grid=(steps,),
+        in_specs=specs,
+        out_specs=specs,
+        out_shape=[jax.ShapeDtypeStruct(a.shape, a.dtype) for a in arrays],
+        compiler_params=params(),
+        name="results",
+    )(*arrays)
 
 
 def solution(mesh):
@@ -465,7 +494,7 @@
         cos_t, sin_t = jnp.cos(angles), jnp.sin(angles)
         mean, rstd, gain = ln_mean[None, :], ln_rstd[None, :], ln_gain[None, :]
         normed, *qkv, stat = qkv_call(resid_x, mean, rstd, gain, w_qkv, cos_t, sin_t)
-        grad_x, gw_up, gw_qkv, gw_down, gw_out = layer_call(mesh, qkv, stat, resid_x, normed, grad_y, w_out, w_up, w_down, w_qkv, gain, cos_t, sin_t)
+        grad_x, gw_up, gw_qkv, gw_down, gw_out = copy_call(layer_call(mesh, qkv, stat, resid_x, normed, grad_y, w_out, w_up, w_down, w_qkv, gain, cos_t, sin_t))
         return grad_x, gw_qkv, gw_out, gw_up, gw_down
 
     in_specs = (P("data", None), P("data"), P("data"), P(None), P("data", None), P(None, "model"), P("model", None, None), P(None, "model"), P("model", None))

time: 290 us -> 274 us (0.945)
  local copies, waits for them, and re-layouts: 21.6 us -> 1.29 us
  Pallas kernels: 265 us -> 270 us
    unnamed x13 -> x0, local copies, waits for them, and re-layouts: 20.3 us -> none
    pallas_call x0 -> x1, Pallas kernels: none -> 16.9 us  [copy_call(): pl.pallas_call(copy_kernel, grid=(steps,), in_specs=specs, out_specs=spec...]
    pallas_call x1, Pallas kernels: 245 us -> 235 us  [layer_call(): pl.pallas_call(functools.partial(layer_kernel, nb, nz), grid=(nb + 5,), i...]
where the time goes in v5:
time: 274 us
  Pallas kernels  270 us (99%)
    pallas_call x1, Pallas kernels, layer_call(): pl.pallas_call(functools.partial(layer_kernel, nb, nz), grid=(nb + 5,), i...  235 us
    pallas_call x1, Pallas kernels, qkv_call(): pl.pallas_call(qkv_kernel, grid=(t // BLK,), in_specs=[rows(d), lanes(1),...  17.6 us
    pallas_call x1, Pallas kernels, copy_call(): pl.pallas_call(copy_kernel, grid=(steps,), in_specs=specs, out_specs=spec...  16.9 us

profile of v5, /device:TPU:21, one launch (start us, length us, event | category | flops | bytes accessed | tf_op | source)
XLA Modules:
  0.0 273.6 jit_solution(12377007025055927468)
XLA Ops:
  0.6 1.3 broadcast_in_dim.13.g_ref.gain_ref
  1.9 1.8 fusion
  3.8 17.6 %ln_qkv.1 = (bf16[4096,2048]{1,0:T(8,128)(2,1)}, bf16[4096,128]{1,0:T(8,128)(2,1)}, bf16[4096,128]{1,0:T(8,128)(2,1)}, bf16[4096,128]{1,0:T(8,128)(2,1)}, bf16[1...) custom-call(bf16[4096,2048]{1,0:T(8,128)(2,1)} %x_hbm.1, f32[1,4096]{1,0:T(1,128)} %bitcast.2, ...), custom_call_target="tpu_custom_call" | custom-call | flops 6442450944 | bytes 33554432 | tf_op jit(solution)/shard_map/ln_qkv/pallas_call | solution.py:87
  21.4 235.2 %layer_backward.1 = (bf16[4096,2048]{1,0:T(8,128)(2,1)}, bf16[2048,512]{1,0:T(8,128)(2,1)}, bf16[2048,384]{1,0:T(8,128)(2,1)}, bf16[512,2048]{1,0:T(8,128)(2,1)}, bf16[1,128,2048]{2,1,0:T(8,128)(2,1)}) custom-call(bf16[4096,128]{1,0:T(8,128)(2,1)} %get-tuple-element.22.q_ref, bf16[4096,128]{1,0:T(8,128)(2,1)} %get-tuple-element.23.k_ref, ...), custom_call_target="tpu_custom_call" | custom-call | flops 62277025792 | bytes 100663296 | tf_op jit(solution)/shard_map/layer_backward/pallas_call | solution.py:439
  256.6 16.9 %results.1 = (bf16[4096,2048]{1,0:T(8,128)(2,1)}, bf16[2048,512]{1,0:T(8,128)(2,1)}, bf16[2048,384]{1,0:T(8,128)(2,1)}, bf16[512,2048]{1,0:T(8,128)(2,1)}, bf16[1,128,2048]{2,1,0:T(8,128)(2,1)}) custom-call(bf16[4096,2048]{1,0:T(8,128)(2,1)} %get-tuple-element.29.refs_0_, bf16[2048,512]{1,0:T(8,128)(2,1)} %get-tuple-element.30.refs_1_, ...), custom_call_target="tpu_custom_call" | custom-call | tf_op jit(solution)/shard_map/results/pallas_call | solution.py:475
  (1 shorter events, 0.0 us)

commit v6 on v5

--- a/solution.py
+++ b/solution.py
@@ -15,7 +15,7 @@
 CORES = 2
 LOG2E = 1.4426950408889634
 TICKS = 10
-PUT_OFF = 2
+PUT_OFF = 3
 OFFSET = 3
 
 

time: 274 us -> 270 us (0.985)
  Pallas kernels: 270 us -> 266 us
    pallas_call x1, Pallas kernels: 235 us -> 231 us  [layer_call(): pl.pallas_call(functools.partial(layer_kernel, nb, nz), grid=(nb + 5,), i...]
where the time goes in v6:
time: 270 us
  Pallas kernels  266 us (99%)
    pallas_call x1, Pallas kernels, layer_call(): pl.pallas_call(functools.partial(layer_kernel, nb, nz), grid=(nb + 5,), i...  231 us
    pallas_call x1, Pallas kernels, qkv_call(): pl.pallas_call(qkv_kernel, grid=(t // BLK,), in_specs=[rows(d), lanes(1),...  17.6 us
    pallas_call x1, Pallas kernels, copy_call(): pl.pallas_call(copy_kernel, grid=(steps,), in_specs=specs, out_specs=spec...  16.9 us

profile of v6, /device:TPU:21, one launch (start us, length us, event | category | flops | bytes accessed | tf_op | source)
XLA Modules:
  0.0 269.6 jit_solution(15799686473721468830)
XLA Ops:
  0.6 1.3 broadcast_in_dim.13.g_ref.gain_ref
  1.9 1.8 fusion
  3.8 17.6 %ln_qkv.1 = (bf16[4096,2048]{1,0:T(8,128)(2,1)}, bf16[4096,128]{1,0:T(8,128)(2,1)}, bf16[4096,128]{1,0:T(8,128)(2,1)}, bf16[4096,128]{1,0:T(8,128)(2,1)}, bf16[1...) custom-call(bf16[4096,2048]{1,0:T(8,128)(2,1)} %x_hbm.1, f32[1,4096]{1,0:T(1,128)} %bitcast.2, ...), custom_call_target="tpu_custom_call" | custom-call | flops 6442450944 | bytes 33554432 | tf_op jit(solution)/shard_map/ln_qkv/pallas_call | solution.py:87
  21.4 231.1 %layer_backward.1 = (bf16[4096,2048]{1,0:T(8,128)(2,1)}, bf16[2048,512]{1,0:T(8,128)(2,1)}, bf16[2048,384]{1,0:T(8,128)(2,1)}, bf16[512,2048]{1,0:T(8,128)(2,1)}, bf16[1,128,2048]{2,1,0:T(8,128)(2,1)}) custom-call(bf16[4096,128]{1,0:T(8,128)(2,1)} %get-tuple-element.22.q_ref, bf16[4096,128]{1,0:T(8,128)(2,1)} %get-tuple-element.23.k_ref, ...), custom_call_target="tpu_custom_call" | custom-call | flops 62277025792 | bytes 100663296 | tf_op jit(solution)/shard_map/layer_backward/pallas_call | solution.py:439
  252.5 16.9 %results.1 = (bf16[4096,2048]{1,0:T(8,128)(2,1)}, bf16[2048,512]{1,0:T(8,128)(2,1)}, bf16[2048,384]{1,0:T(8,128)(2,1)}, bf16[512,2048]{1,0:T(8,128)(2,1)}, bf16[1,128,2048]{2,1,0:T(8,128)(2,1)}) custom-call(bf16[4096,2048]{1,0:T(8,128)(2,1)} %get-tuple-element.29.refs_0_, bf16[2048,512]{1,0:T(8,128)(2,1)} %get-tuple-element.30.refs_1_, ...), custom_call_target="tpu_custom_call" | custom-call | tf_op jit(solution)/shard_map/results/pallas_call | solution.py:475
  (1 shorter events, 0.0 us)
